TPU v7x, 64 devices: a 2x2x8 block of a 4x4x8 slice. The times are simulated.
64 devices in a mesh: dp: 4 (over x, y), tp: 16 (over z, core).
Axes of the slice: x: 2, y: 2, z: 8, core: 2. Of those that a mesh axis runs over, the one named last changes fastest.
The devices are a block of a 4x4x8 slice.
Arguments:
- token_ids: int32 [32768], P('dp'), parts along dimension 0
- emb_table: bfloat16 [32128, 512], P('tp')
- norm_gain: bfloat16 [512], replicated
- w_in: bfloat16 [512, 2048], P(None, 'tp')
- w_out: bfloat16 [2048, 512], P('tp')
- d_out: bfloat16 [32768, 512], P(('dp', 'tp')), parts along dimension 0
Outputs:
- output 1: bfloat16 [32768, 512], P(('dp', 'tp')), parts along dimension 0
- output 2: float32 [128512, 512], P(('dp', 'tp')), parts along dimension 0
- output 3: float32 [2048, 2048], P('dp', 'tp'), parts along dimension 0
- output 4: float32 [8192, 512], P(('dp', 'tp')), parts along dimension 0
There are 4 independent parts. A program takes and returns all parts, laid end to end along the dimension named above; an argument that names none is the same for every part.
All inputs are finite; a program needn't handle non-finite values.
Results may differ from a plain program's by a relative error of at most 0.00935178.
Values are sent between devices in bfloat16 or wider.
A program may use at most 768 MiB of HBM per device.

v0:
```python
import jax
import jax.numpy as jnp
from jax import lax
from jax.sharding import PartitionSpec as P

EPS = 1e-6


def solution(mesh):
    def shard_step(token_ids, emb_table, norm_gain, w_in, w_out, d_out):
        shard_rank = lax.axis_index("tp")
        vocab_local = emb_table.shape[0]
        local_ids = token_ids - shard_rank * vocab_local
        is_owned = (local_ids >= 0) & (local_ids < vocab_local)
        table_rows = jnp.take(emb_table, jnp.where(is_owned, local_ids, 0), axis=0)
        lookup_part = jnp.where(is_owned[:, None], table_rows, jnp.zeros((), table_rows.dtype))
        embedded = lax.psum_scatter(lookup_part, "tp", scatter_dimension=0, tiled=True)
        embedded_f32 = embedded.astype(jnp.float32)
        inv_rms = lax.rsqrt(jnp.mean(embedded_f32 * embedded_f32, axis=-1, keepdims=True) + EPS)
        gain_f32 = norm_gain.astype(jnp.float32)
        normed_local = (embedded_f32 * inv_rms * gain_f32).astype(jnp.bfloat16)
        normed = lax.all_gather(normed_local, "tp", axis=0, tiled=True)
        pre_act = jnp.dot(normed, w_in, preferred_element_type=jnp.float32).astype(jnp.bfloat16)
        act_f32, gelu_vjp = jax.vjp(jax.nn.gelu, pre_act.astype(jnp.float32))
        hidden = act_f32.astype(jnp.bfloat16)
        mlp_part = jnp.dot(hidden, w_out, preferred_element_type=jnp.float32)
        mlp_out = lax.psum_scatter(mlp_part, "tp", scatter_dimension=0, tiled=True)
        block_out = (embedded_f32 + mlp_out).astype(jnp.bfloat16)

        d_out_full = lax.all_gather(d_out, "tp", axis=0, tiled=True)
        d_hidden = lax.dot_general(d_out_full, w_out, (((1,), (1,)), ((), ())), preferred_element_type=jnp.float32).astype(jnp.bfloat16)
        d_w_out = lax.dot_general(hidden, d_out_full, (((0,), (0,)), ((), ())), preferred_element_type=jnp.float32)
        (d_pre_f32,) = gelu_vjp(d_hidden.astype(jnp.float32))
        d_pre = d_pre_f32.astype(jnp.bfloat16)
        d_w_in = lax.dot_general(normed, d_pre, (((0,), (0,)), ((), ())), preferred_element_type=jnp.float32)
        d_norm_part = lax.dot_general(d_pre, w_in, (((1,), (1,)), ((), ())), preferred_element_type=jnp.float32)
        d_normed = lax.psum_scatter(d_norm_part, "tp", scatter_dimension=0, tiled=True)
        d_scaled = d_normed * gain_f32
        row_proj = jnp.mean(d_scaled * embedded_f32, axis=-1, keepdims=True)
        d_emb = (d_out.astype(jnp.float32) + inv_rms * (d_scaled - embedded_f32 * inv_rms * inv_rms * row_proj)).astype(jnp.bfloat16)
        d_emb_full = lax.all_gather(d_emb, "tp", axis=0, tiled=True)
        target_rows = jnp.where(is_owned, local_ids, vocab_local)
        d_table = jax.ops.segment_sum(d_emb_full.astype(jnp.float32), target_rows, num_segments=vocab_local)
        return block_out, d_table, d_w_in, d_w_out

    return jax.shard_map(
        shard_step,
        mesh=mesh,
        in_specs=(P("dp"), P("tp", None), P(None), P(None, "tp"), P("tp", None), P(("dp", "tp"), None)),
        out_specs=(P(("dp", "tp"), None), P(("dp", "tp"), None), P("dp", "tp"), P(("dp", "tp"), None)),
        check_vma=False,
    )
```

profile of v0, /device:TPU:21, one launch (start us, length us, event | category | flops | bytes accessed | tf_op | source)
XLA Modules:
  0.0 556.2 jit_solution(6568257222616697645)
XLA Ops:
  7.2 0.1 reduce-scatter.4.cloned.1.call-start
  7.3 0.9 compare_and_fusion.1
  8.2 0.8 subtract_select_fusion
  9.0 33.7 %gather_fusion = bf16[8192,512]{1,0:T(8,128)(2,1)} fusion(bf16[2008,512]{1,0:T(8,128)(2,1)S(1)} %copy-done, s32[8192]{0:T(1024)S(1)} %get-tuple-element.7), kind=kCustom, calls=%fused_computation | custom fusion | bytes 16809984 | tf_op jit(solution)/shard_map/jit(_take)/gather | solution.py:15
  42.7 8.2 %select_select_fusion = bf16[8192,512]{1,0:T(8,128)(2,1)} fusion(bf16[8192,512]{1,0:T(8,128)(2,1)} %gather_fusion, pred[8192]{0:T(1024)(128)(4,1)S(1)} %get-tuple-element.9, pred[8192]{0:T(1024)(128)(4,1)S(1)} %get-tuple-element.8), kind=kLoop, calls=%fused_computation.8 | loop fusion | flops 8388608 | bytes 16793600 | tf_op jit(solution)/shard_map/jit(_where)/select_n | solution.py:16
  50.9 0.1 all-gather.4.cloned.1.call-start
  51.0 0.5 copy-done.8
  51.5 68.8 %reduce-scatter.4.cloned.1.call-done = bf16[512,512]{1,0:T(8,128)(2,1)} async-done(((bf16[8192,512]{1,0:T(8,128)(2,1)}), bf16[512,512]{1,0:T(8,128)(2,1)}) %reduce-scatter.4.cloned.1.call-update) | async-done | bytes 524304 | tf_op jit(solution)/shard_map/reduce_scatter | solution.py:17
  120.3 1.2 fusion.20
  121.6 2.0 fusion.14
  123.6 0.1 all-gather.4.cloned.1.call-update
  123.7 0.1 all-gather.6.cloned.1.call-start
  123.7 0.7 all-gather.6.cloned.1.call-update
  124.5 0.1 reduce-scatter.8.cloned.1.call-start
  124.5 53.9 %all-gather.4.cloned.1.call-done = bf16[8192,512]{1,0:T(8,128)(2,1)} async-done(((bf16[512,512]{1,0:T(8,128)(2,1)}), bf16[8192,512]{1,0:T(8,128)(2,1)}) %all-gather.4.cloned.1.call-update) | async-done | bytes 8388624 | tf_op jit(solution)/shard_map/all_gather | solution.py:22
  178.4 7.8 %fusion.3 = f32[8192,128]{1,0:T(8,128)} fusion(bf16[8192,512]{1,0:T(8,128)(2,1)} %all-gather.4.cloned.1.call-done, bf16[512,128]{1,0:T(8,128)(2,1)S(1)} %copy-done.6), kind=kOutput, calls=%fused_computation.7 | convolution fusion | flops 1075838976 | bytes 12713984 | tf_op jit(solution)/shard_map/dot_general | solution.py:23
  186.2 44.9 %all-gather.6.cloned.1.call-done = bf16[8192,512]{1,0:T(8,128)(2,1)} async-done(((bf16[512,512]{1,0:T(8,128)(2,1)}), bf16[8192,512]{1,0:T(8,128)(2,1)}) %all-gather.6.cloned.1.call-update) | async-done | bytes 8388624 | tf_op jit(solution)/shard_map/all_gather | solution.py:30
  231.1 7.9 %fusion.10 = bf16[8192,128]{1,0:T(8,128)(2,1)S(1)} fusion(f32[8192,128]{1,0:T(8,128)} %fusion.3, bf16[8192,512]{1,0:T(8,128)(2,1)} %all-gather.6.cloned.1.call-done, bf16[128,512]{1,0:T(8,128)(2,1)S(1)} %copy-done.7), kind=kOutput, calls=%fused_computation.17 | convolution fusion | flops 1096810496 | bytes 14811136 | tf_op jit(solution)/shard_map/dot_general | solution.py:31
  239.0 1.3 copy-done.3
  240.4 8.1 %fusion.26 = f32[8192,512]{1,0:T(8,128)} fusion(bf16[8192,128]{1,0:T(8,128)(2,1)S(1)} %fusion.10, bf16[512,128]{1,0:T(8,128)(2,1)S(1)} %copy-done.6), kind=kOutput, calls=%fused_computation.44 | convolution fusion | flops 1073741824 | bytes 19005440 | tf_op jit(solution)/shard_map/dot_general | solution.py:36
  248.5 0.2 reduce-scatter.6.cloned.1.call-start
  248.8 10.3 %fusion.25 = f32[8192,512]{1,0:T(8,128)} fusion(bf16[128,512]{1,0:T(8,128)(2,1)S(1)} %copy-done.7, f32[8192,128]{1,0:T(8,128)} %fusion.3), kind=kOutput, calls=%fused_computation.43 | convolution fusion | flops 1083179008 | bytes 21102592 | tf_op jit(solution)/shard_map/dot_general | solution.py:26
  259.1 0.1 all-gather.8.cloned.1.call-start
  259.2 84.3 %reduce-scatter.8.cloned.1.call-done = f32[512,512]{1,0:T(8,128)} async-done(((f32[8192,512]{1,0:T(8,128)}), f32[512,512]{1,0:T(8,128)}) %reduce-scatter.8.cloned.1.call-update) | async-done | bytes 1048592 | tf_op jit(solution)/shard_map/reduce_scatter | solution.py:37
  343.5 1.4 fusion.22
  344.9 96.7 %reduce-scatter.6.cloned.1.call-done = f32[512,512]{1,0:T(8,128)} async-done(((f32[8192,512]{1,0:T(8,128)}), f32[512,512]{1,0:T(8,128)}) %reduce-scatter.6.cloned.1.call-update) | async-done | bytes 1048592 | tf_op jit(solution)/shard_map/reduce_scatter | solution.py:27
  441.7 2.9 fusion.19
  444.6 0.1 all-gather.8.cloned.1.call-update
  444.7 7.5 %fusion.24 = f32[128,512]{1,0:T(8,128)} fusion(bf16[8192,512]{1,0:T(8,128)(2,1)} %all-gather.6.cloned.1.call-done, f32[8192,128]{1,0:T(8,128)} %fusion.3), kind=kOutput, calls=%fused_computation.42 | convolution fusion | flops 1083179008 | bytes 12845056 | tf_op jit(solution)/shard_map/dot_general | solution.py:32
  452.2 6.4 %fusion.27 = f32[512,128]{1,0:T(8,128)} fusion(bf16[8192,512]{1,0:T(8,128)(2,1)} %all-gather.4.cloned.1.call-done, bf16[8192,128]{1,0:T(8,128)(2,1)S(1)} %copy-done.4), kind=kOutput, calls=%fused_computation.45 | convolution fusion | flops 1073741824 | bytes 10747904 | tf_op jit(solution)/shard_map/dot_general | solution.py:35
  458.6 38.4 %all-gather.8.cloned.1.call-done = bf16[8192,512]{1,0:T(8,128)(2,1)} async-done(((bf16[512,512]{1,0:T(8,128)(2,1)}), bf16[8192,512]{1,0:T(8,128)(2,1)}) %all-gather.8.cloned.1.call-update) | async-done | bytes 8388624 | tf_op jit(solution)/shard_map/all_gather | solution.py:41
  497.0 52.3 %scatter_custom_fusion = f32[2008,512]{1,0:T(8,128)} fusion(s32[8192]{0:T(1024)S(1)} %get-tuple-element.6, bf16[8192,512]{1,0:T(8,128)(2,1)} %all-gather.8.cloned.1.call-done, f32[]{:T(128)} %constant.21.clone.1), kind=kCustom, calls=%fused_computation.2 | custom fusion | flops 8388608 | bytes 12500996 | tf_op jit(solution)/shard_map/scatter-add | solution.py:43
  (22 shorter events, 0.2 us)
Async XLA Ops:
  7.2 1.8 copy-start
  7.2 113.2 %reduce-scatter.4.cloned.1.call-start = ((), (), s32[]{:S(2)}) async-start(), calls=%async_computation.3 | async-start | bytes 8912896 | tf_op jit(solution)/shard_map/reduce_scatter | solution.py:17
  50.8 0.7 copy-start.8
  50.8 127.6 %copy-start.6 = (bf16[512,128]{1,0:T(8,128)(2,1)S(1)}, bf16[512,128]{1,0:T(8,128)(2,1)}, u32[]{:S(2)}) copy-start(bf16[512,128]{1,0:T(8,128)(2,1)} %param.9) | copy-start | bytes 393220
  50.9 127.5 %all-gather.4.cloned.1.call-start = ((), (), s32[]{:S(2)}) async-start(), calls=%async_computation.4 | async-start | bytes 8912896 | tf_op jit(solution)/shard_map/all_gather | solution.py:22
  123.7 107.5 %all-gather.6.cloned.1.call-start = ((), (), s32[]{:S(2)}) async-start(), calls=%async_computation.6 | async-start | bytes 8912896 | tf_op jit(solution)/shard_map/all_gather | solution.py:30
  124.5 106.7 %copy-start.7 = (bf16[128,512]{1,0:T(8,128)(2,1)S(1)}, bf16[128,512]{1,0:T(8,128)(2,1)}, u32[]{:S(2)}) copy-start(bf16[128,512]{1,0:T(8,128)(2,1)} %param.10) | copy-start | bytes 393220
  124.5 219.0 %reduce-scatter.8.cloned.1.call-start = ((), (), s32[]{:S(2)}) async-start(), calls=%async_computation.7 | async-start | bytes 17825792 | tf_op jit(solution)/shard_map/reduce_scatter | solution.py:37
  239.0 1.3 copy-start.3
  248.5 193.2 %reduce-scatter.6.cloned.1.call-start = ((), (), s32[]{:S(2)}) async-start(), calls=%async_computation.5 | async-start | bytes 17825792 | tf_op jit(solution)/shard_map/reduce_scatter | solution.py:27
  259.0 84.5 %copy-start.2 = (bf16[512,512]{1,0:T(8,128)(2,1)S(1)}, bf16[512,512]{1,0:T(8,128)(2,1)}, u32[]{:S(2)}) copy-start(bf16[512,512]{1,0:T(8,128)(2,1)} %reduce-scatter.4.cloned.1.call-done) | copy-start | bytes 1572868
  259.0 182.6 %copy-start.5 = (bf16[512,512]{1,0:T(8,128)(2,1)S(1)}, bf16[512,512]{1,0:T(8,128)(2,1)}, u32[]{:S(2)}) copy-start(bf16[512,512]{1,0:T(8,128)(2,1)} %param.11) | copy-start | bytes 1572868
  259.1 237.9 %all-gather.8.cloned.1.call-start = ((), (), s32[]{:S(2)}) async-start(), calls=%async_computation.8 | async-start | bytes 8912896 | tf_op jit(solution)/shard_map/all_gather | solution.py:41
  444.7 7.5 %copy-start.4 = (bf16[8192,128]{1,0:T(8,128)(2,1)S(1)}, bf16[8192,128]{1,0:T(8,128)(2,1)}, u32[]{:S(2)}) copy-start(bf16[8192,128]{1,0:T(8,128)(2,1)} %copy-done.3) | copy-start | bytes 6291460
  497.0 52.3 %copy-start.1 = (bf16[2008,512]{1,0:T(8,128)(2,1)S(1)}, bf16[2008,512]{1,0:T(8,128)(2,1)}, u32[]{:S(2)}) copy-start(bf16[2008,512]{1,0:T(8,128)(2,1)} %param.7) | copy-start | bytes 6168580
Sparse Core Ops, SparseCore 0:
  51.0 69.2 reduce-scatter.3
  123.8 54.5 all-gather.3
  180.1 51.0 all-gather.5
  248.6 94.8 reduce-scatter.7
  345.7 95.9 reduce-scatter.5
  444.8 52.1 all-gather.7
where the time goes:
time: 557 us; the launch traced here: 556 us
  waiting for transfers between devices  388 us (70%)
  other arithmetic  69.8 us (13%)
  matrix products  48 us (9%)
  local copies, waits for them, and re-layouts  35.6 us (6%)
  between operations  14.2 us (3%)
    reduce_scatter x1, waiting for transfers between devices, shard_step(): mlp_out = lax.psum_scatter(mlp_part, 'tp', scatter_dimension=0, tiled=True)  96.7 us
    reduce_scatter x1, waiting for transfers between devices, shard_step(): lax.psum_scatter(d_norm_part, 'tp', scatter_dimension=0, tiled=True)  84.3 us
    reduce_scatter x1, waiting for transfers between devices, shard_step(): lax.psum_scatter(lookup_part, 'tp', scatter_dimension=0, tiled=True)  68.8 us
    all_gather x1, waiting for transfers between devices, shard_step(): normed = lax.all_gather(normed_local, 'tp', axis=0, tiled=True)  53.9 us
    scatter-add x1, other arithmetic, shard_step(): jax.ops.segment_sum(d_emb_full.astype(jnp.float32), target_rows, num_segm...  52.3 us
    all_gather x1, waiting for transfers between devices, shard_step(): d_out_full = lax.all_gather(d_out, 'tp', axis=0, tiled=True)  44.9 us
    all_gather x1, waiting for transfers between devices, shard_step(): d_emb_full = lax.all_gather(d_emb, 'tp', axis=0, tiled=True)  38.4 us
    gather x1, local copies, waits for them, and re-layouts, shard_step(): table_rows = jnp.take(emb_table, jnp.where(is_owned, local_ids, 0), axis=0)  33.7 us
  transfers between devices with their start and end apart: 6, of which 6 were waited for; matrix products, arithmetic and copies ran while one was open for 6% of the time, Pallas kernels for 0%

commit v1 on v0

v1 whole, which is shorter than its diff:
```python
import jax
import jax.numpy as jnp
from jax import lax
from jax.sharding import PartitionSpec as P

EPS = 1e-6


def solution(mesh):
    tp = mesh.shape["tp"]

    def shard_step(token_ids, emb_table, norm_gain, w_in, w_out, d_out):
        f32, bf16 = jnp.float32, jnp.bfloat16
        rank = lax.axis_index("tp")
        vocab_local, dim = emb_table.shape
        hid = w_out.shape[0]
        local_ids = token_ids - rank * vocab_local
        weights = lax.all_gather(jnp.concatenate([w_in.T, w_out], axis=0), "tp", axis=0, tiled=False)
        w_in_t = weights[:, :hid].reshape(tp * hid, dim)
        w_out_full = weights[:, hid:].reshape(tp * hid, dim)
        pick = (local_ids[:, None] == lax.broadcasted_iota(jnp.int32, (token_ids.shape[0], vocab_local), 1)).astype(bf16)
        lookup_part = jnp.dot(pick, emb_table, preferred_element_type=f32).astype(bf16)
        embedded = lax.psum_scatter(lookup_part, "tp", scatter_dimension=0, tiled=True)
        x = embedded.astype(f32)
        inv_rms = lax.rsqrt(jnp.mean(x * x, axis=-1, keepdims=True) + EPS)
        gain = norm_gain.astype(f32)
        normed = (x * inv_rms * gain).astype(bf16)
        pre_act = lax.dot_general(normed, w_in_t, (((1,), (1,)), ((), ())), preferred_element_type=f32).astype(bf16)
        act, gelu_vjp = jax.vjp(jax.nn.gelu, pre_act.astype(f32))
        hidden = act.astype(bf16)
        y = jnp.dot(hidden, w_out_full, preferred_element_type=f32)
        block_out = (x + y).astype(bf16)

        d_hidden = lax.dot_general(d_out, w_out_full, (((1,), (1,)), ((), ())), preferred_element_type=f32).astype(bf16)
        (d_pre_f32,) = gelu_vjp(d_hidden.astype(f32))
        d_pre = d_pre_f32.astype(bf16)
        d_normed = jnp.dot(d_pre, w_in_t, preferred_element_type=f32)
        d_scaled = d_normed * gain
        row_proj = jnp.mean(d_scaled * x, axis=-1, keepdims=True)
        d_emb = (d_out.astype(f32) + inv_rms * (d_scaled - x * inv_rms * inv_rms * row_proj)).astype(bf16)
        d_emb_full = lax.all_gather(d_emb, "tp", axis=0, tiled=True)
        d_w_out_part = lax.dot_general(hidden, d_out, (((0,), (0,)), ((), ())), preferred_element_type=f32)
        d_w_in_part = lax.dot_general(d_pre, normed, (((0,), (0,)), ((), ())), preferred_element_type=f32)
        d_w_part = jnp.concatenate([d_w_in_part.reshape(tp, hid, dim), d_w_out_part.reshape(tp, hid, dim)], axis=1)
        d_w = lax.psum_scatter(d_w_part.reshape(tp * 2 * hid, dim), "tp", scatter_dimension=0, tiled=True)
        d_w_in = d_w[:hid].T
        d_w_out = d_w[hid:]
        place = (lax.broadcasted_iota(jnp.int32, (vocab_local, token_ids.shape[0]), 0) == local_ids[None, :]).astype(bf16)
        d_table = jnp.dot(place, d_emb_full, preferred_element_type=f32)
        return block_out, d_table, d_w_in, d_w_out

    return jax.shard_map(
        shard_step,
        mesh=mesh,
        in_specs=(P("dp"), P("tp", None), P(None), P(None, "tp"), P("tp", None), P(("dp", "tp"), None)),
        out_specs=(P(("dp", "tp"), None), P(("dp", "tp"), None), P("dp", "tp"), P(("dp", "tp"), None)),
        check_vma=False,
    )
```

time: 557 us -> 262 us (0.47)
  waiting for transfers between devices: 388 us -> 163 us
  other arithmetic: 69.8 us -> 9.62 us
  local copies, waits for them, and re-layouts: 35.6 us -> 10.4 us
  matrix products: 48 us -> 61.9 us
    reduce_scatter x2 -> x1, waiting for transfers between devices: 181 us -> 40.8 us  [shard_step(): lax.psum_scatter(d_w_part.reshape(tp * 2 * hid, dim), 'tp', scatter_dimen...]
    all_gather x2 -> x1, waiting for transfers between devices: 98.8 us -> 22.5 us  [shard_step(): lax.all_gather(jnp.concatenate([w_in.T, w_out], axis=0), 'tp', axis=0, ti...]
    scatter-add x1 -> x0, other arithmetic: 52.3 us -> none  [shard_step(): jax.ops.segment_sum(d_emb_full.astype(jnp.float32), target_rows, num_segm...]
    gather x1 -> x0, local copies, waits for them, and re-layouts: 33.7 us -> none  [shard_step(): table_rows = jnp.take(emb_table, jnp.where(is_owned, local_ids, 0), axis=0)]
    dot_general x6 -> x8, matrix products: 48 us -> 61.9 us  [the longest x1 24.1 us: shard_step(): d_table = jnp.dot(place, d_emb_full, preferred_element_type=f32)]
    select_n x2 -> x0, other arithmetic: 8.95 us -> none  [the longest x1 8.17 us: shard_step(): jnp.where(is_owned[:, None], table_rows, jnp.zeros((), table_rows.dtype))]
    reduce_scatter x1, waiting for transfers between devices: 68.8 us -> 60.2 us  [shard_step(): lax.psum_scatter(lookup_part, 'tp', scatter_dimension=0, tiled=True)]
    slice x0 -> x2, local copies, waits for them, and re-layouts: none -> 6.45 us  [the longest x1 4.68 us: shard_step(): w_in_t = weights[:, :hid].reshape(tp * hid, dim)]
  transfers between devices with their start and end apart: 6 -> 4, of which waited for: 6 -> 4; matrix products, arithmetic and copies ran while one was open for 6% -> 25% of each run, Pallas kernels for 0% -> 0%
where the time goes in v1:
time: 262 us; the launch traced here: 260 us
  waiting for transfers between devices  163 us (62%)
  matrix products  61.9 us (24%)
  between operations  13.9 us (5%)
  local copies, waits for them, and re-layouts  10.4 us (4%)
  other arithmetic  9.62 us (4%)
    reduce_scatter x1, waiting for transfers between devices, shard_step(): lax.psum_scatter(lookup_part, 'tp', scatter_dimension=0, tiled=True)  60.2 us
    reduce_scatter x1, waiting for transfers between devices, shard_step(): lax.psum_scatter(d_w_part.reshape(tp * 2 * hid, dim), 'tp', scatter_dimen...  40.8 us
    all_gather x1, waiting for transfers between devices, shard_step(): d_emb_full = lax.all_gather(d_emb, 'tp', axis=0, tiled=True)  39.7 us
    dot_general x1, matrix products, shard_step(): d_table = jnp.dot(place, d_emb_full, preferred_element_type=f32)  24.1 us
    all_gather x1, waiting for transfers between devices, shard_step(): lax.all_gather(jnp.concatenate([w_in.T, w_out], axis=0), 'tp', axis=0, ti...  22.5 us
    dot_general x1, matrix products, shard_step(): jnp.dot(pick, emb_table, preferred_element_type=f32).astype(bf16)  19.8 us
  transfers between devices with their start and end apart: 4, of which 4 were waited for; matrix products, arithmetic and copies ran while one was open for 25% of the time, Pallas kernels for 0%

profile of v1, /device:TPU:21, one launch (start us, length us, event | category | flops | bytes accessed | tf_op | source)
XLA Modules:
  0.0 259.7 jit_solution(9008972431654777425)
XLA Ops:
  7.2 0.0 copy-start
  7.2 0.1 all-gather.6.cloned.1.call-start
  7.3 1.1 copy.14
  8.4 1.6 pad_maximum_fusion.1
  10.0 0.1 all-gather.6.cloned.1.call-update
  10.1 0.1 reduce-scatter.3.cloned.1.call-start
  10.2 0.8 broadcast_subtract_fusion
  10.9 19.8 %fusion.4 = bf16[8192,512]{1,0:T(8,128)(2,1)} fusion(bf16[2008,512]{1,0:T(8,128)(2,1)S(1)} %copy-done, s32[8192]{0:T(1024)S(1)} %broadcast_subtract_fusion), kind=kOutput, calls=%fused_computation.6 | convolution fusion | flops 16864968704 | bytes 10477568 | tf_op jit(solution)/shard_map/dot_general | solution.py:22
  30.8 0.1 reduce-scatter.3.cloned.1.call-update
  30.8 0.1 all-gather.4.cloned.1.call-start
  30.9 0.5 copy-done.6
  31.5 22.5 %all-gather.6.cloned.1.call-done = bf16[4096,512]{1,0:T(8,128)(2,1)} async-done(((bf16[256,512]{1,0:T(8,128)(2,1)}), bf16[4096,512]{1,0:T(8,128)(2,1)}) %all-gather.6.cloned.1.call-update) | async-done | bytes 4194320 | tf_op jit(solution)/shard_map/all_gather | solution.py:18
  54.0 4.7 %fusion.33 = (bf16[16,128,512]{2,1,0:T(8,128)(2,1)}, bf16[16,128,512]{2,1,0:T(8,128)(2,1)}) fusion(bf16[16,256,512]{2,1,0:T(8,128)(2,1)} %bitcast.30), kind=kLoop, calls=%fused_computation.50 | loop fusion | bytes 8388608 | tf_op jit(solution)/shard_map/slice | solution.py:19
  58.6 60.2 %reduce-scatter.3.cloned.1.call-done = bf16[512,512]{1,0:T(8,128)(2,1)} async-done(((bf16[8192,512]{1,0:T(8,128)(2,1)}), bf16[512,512]{1,0:T(8,128)(2,1)}) %reduce-scatter.3.cloned.1.call-update) | async-done | bytes 524304 | tf_op jit(solution)/shard_map/reduce_scatter | solution.py:23
  118.8 1.2 fusion.25
  120.1 3.2 %convolution_convert_fusion.1 = bf16[512,2048]{1,0:T(8,128)(2,1)S(1)} fusion(bf16[2048,512]{1,0:T(8,128)(2,1)} %bitcast.34, bf16[512,512]{1,0:T(8,128)(2,1)} %reduce-scatter.3.cloned.1.call-done, f32[512]{0:T(512)S(1)} %convert_element_type.47, f32[512]{0:T(512)S(1)} %add_rsqrt_fusion), kind=kOutput, calls=%fused_computation.26 | convolution fusion | flops 1075838976 | bytes 4722688 | tf_op jit(solution)/shard_map/dot_general | solution.py:28
  123.3 3.6 %fusion.8 = bf16[512,2048]{1,0:T(8,128)(2,1)S(1)} fusion(bf16[512,2048]{1,0:T(8,128)(2,1)S(1)} %convolution_convert_fusion.1, bf16[2048,512]{1,0:T(8,128)(2,1)S(1)} %bitcast.33, bf16[512,512]{1,0:T(8,128)(2,1)S(1)} %copy-done.5), kind=kOutput, calls=%fused_computation.16 | convolution fusion | flops 1097859072 | bytes 6815744 | tf_op jit(solution)/shard_map/dot_general | solution.py:34
  127.0 1.4 copy-done.2
  128.3 1.3 fusion.26
  129.7 1.2 fusion.24
  130.8 0.1 all-gather.4.cloned.1.call-update
  130.9 0.2 reduce-scatter.5.cloned.1.call-start
  131.2 3.1 %fusion.27 = f32[2048,512]{1,0:T(8,128)S(1)} fusion(bf16[512,2048]{1,0:T(8,128)(2,1)} %copy-done.2, bf16[512,512]{1,0:T(8,128)(2,1)S(1)} %copy-done.1, f32[512]{0:T(512)S(1)} %convert_element_type.47, f32[512]{0:T(512)S(1)} %add_rsqrt_fusion), kind=kOutput, calls=%fused_computation.45 | convolution fusion | flops 1074790400 | bytes 6819840 | tf_op jit(solution)/shard_map/dot_general | solution.py:43
  134.3 2.1 fusion.30
  136.4 4.8 %pad_maximum_fusion = f32[16,256,512]{2,1,0:T(8,128)} fusion(f32[16,128,512]{2,1,0:T(8,128)S(1)} %bitcast.31, f32[16,128,512]{2,1,0:T(8,128)S(1)} %bitcast.29), kind=kLoop, calls=%fused_computation.7 | loop fusion | flops 2097152 | bytes 16777216 | tf_op jit(solution)/shard_map/concatenate | solution.py:44
  141.2 0.1 reduce-scatter.5.cloned.1.call-update
  141.3 4.6 %fusion.16 = bf16[512,512]{1,0:T(8,128)(2,1)} fusion(bf16[2048,512]{1,0:T(8,128)(2,1)} %bitcast.32, bf16[512,512]{1,0:T(8,128)(2,1)S(1)} %copy-done.1, bf16[512,2048]{1,0:T(8,128)(2,1)} %copy-done.7), kind=kOutput, calls=%fused_computation.32 | convolution fusion | flops 1085014016 | bytes 5242880 | tf_op jit(solution)/shard_map/dot_general | solution.py:31
  145.9 39.7 %all-gather.4.cloned.1.call-done = bf16[8192,512]{1,0:T(8,128)(2,1)} async-done(((bf16[512,512]{1,0:T(8,128)(2,1)}), bf16[8192,512]{1,0:T(8,128)(2,1)}) %all-gather.4.cloned.1.call-update) | async-done | bytes 8388624 | tf_op jit(solution)/shard_map/all_gather | solution.py:41
  185.7 24.1 %fusion.1 = f32[2008,512]{1,0:T(8,128)} fusion(bf16[8192,512]{1,0:T(8,128)(2,1)} %all-gather.4.cloned.1.call-done, s32[8192]{0:T(1024)S(1)} %broadcast_subtract_fusion), kind=kOutput, calls=%fused_computation.3 | convolution fusion | flops 16860774400 | bytes 12533760 | tf_op jit(solution)/shard_map/dot_general | solution.py:49
  209.8 40.8 %reduce-scatter.5.cloned.1.call-done = f32[256,512]{1,0:T(8,128)} async-done(((f32[4096,512]{1,0:T(8,128)}), f32[256,512]{1,0:T(8,128)}) %reduce-scatter.5.cloned.1.call-update) | async-done | bytes 524304 | tf_op jit(solution)/shard_map/reduce_scatter | solution.py:45
  250.6 1.8 fusion.34
  252.3 0.8 copy.17
  (18 shorter events, 0.1 us)
Async XLA Ops:
  7.2 3.8 %copy-start = (bf16[2008,512]{1,0:T(8,128)(2,1)S(1)}, bf16[2008,512]{1,0:T(8,128)(2,1)}, u32[]{:S(2)}) copy-start(bf16[2008,512]{1,0:T(8,128)(2,1)} %param.7) | copy-start | bytes 6168580
  7.2 46.8 %all-gather.6.cloned.1.call-start = ((), (), s32[]{:S(2)}) async-start(), calls=%async_computation.5 | async-start | bytes 4456448 | tf_op jit(solution)/shard_map/all_gather | solution.py:18
  10.1 108.7 %reduce-scatter.3.cloned.1.call-start = ((), (), s32[]{:S(2)}) async-start(), calls=%async_computation.2 | async-start | bytes 8912896 | tf_op jit(solution)/shard_map/reduce_scatter | solution.py:23
  30.8 0.7 copy-start.6
  30.8 154.8 %all-gather.4.cloned.1.call-start = ((), (), s32[]{:S(2)}) async-start(), calls=%async_computation.3 | async-start | bytes 8912896 | tf_op jit(solution)/shard_map/all_gather | solution.py:41
  120.0 3.2 %copy-start.3 = (bf16[16,128,512]{2,1,0:T(8,128)(2,1)S(1)}, bf16[16,128,512]{2,1,0:T(8,128)(2,1)}, u32[]{:S(2)}) copy-start(bf16[16,128,512]{2,1,0:T(8,128)(2,1)} %get-tuple-element.13) | copy-start | bytes 6291460
  120.0 3.2 %copy-start.5 = (bf16[512,512]{1,0:T(8,128)(2,1)S(1)}, bf16[512,512]{1,0:T(8,128)(2,1)}, u32[]{:S(2)}) copy-start(bf16[512,512]{1,0:T(8,128)(2,1)} %param.11) | copy-start | bytes 1572868
  123.3 3.7 %copy-start.7 = (bf16[512,2048]{1,0:T(8,128)(2,1)}, bf16[512,2048]{1,0:T(8,128)(2,1)S(1)}, u32[]{:S(2)}) copy-start(bf16[512,2048]{1,0:T(8,128)(2,1)S(1)} %convolution_convert_fusion.1) | copy-start | bytes 6291460
  123.3 5.0 %copy-start.1 = (bf16[512,512]{1,0:T(8,128)(2,1)S(1)}, bf16[512,512]{1,0:T(8,128)(2,1)}, u32[]{:S(2)}) copy-start(bf16[512,512]{1,0:T(8,128)(2,1)} %reduce-scatter.3.cloned.1.call-done) | copy-start | bytes 1572868
  123.3 5.0 %copy-start.4 = (bf16[16,128,512]{2,1,0:T(8,128)(2,1)S(1)}, bf16[16,128,512]{2,1,0:T(8,128)(2,1)}, u32[]{:S(2)}) copy-start(bf16[16,128,512]{2,1,0:T(8,128)(2,1)} %get-tuple-element.12) | copy-start | bytes 6291460
  127.0 1.4 copy-start.2
  130.9 119.6 %reduce-scatter.5.cloned.1.call-start = ((), (), s32[]{:S(2)}) async-start(), calls=%async_computation.4 | async-start | bytes 8912896 | tf_op jit(solution)/shard_map/reduce_scatter | solution.py:45
  131.2 3.1 %copy-start.8 = (bf16[512,2048]{1,0:T(8,128)(2,1)S(1)}, bf16[512,2048]{1,0:T(8,128)(2,1)}, u32[]{:S(2)}) copy-start(bf16[512,2048]{1,0:T(8,128)(2,1)} %copy-done.7) | copy-start | bytes 6291460
Sparse Core Ops, SparseCore 0:
  10.2 43.6 all-gather.5
  56.3 62.4 reduce-scatter.2
  131.0 54.5 all-gather.3
  187.9 62.6 reduce-scatter.4

commit v2 on v0

v2 whole, which is shorter than its diff:
```python
import functools
import math

import jax
import jax.numpy as jnp
from jax import lax
from jax.experimental import pallas as pl
from jax.experimental.pallas import tpu as pltpu
from jax.sharding import PartitionSpec as P

EPS = 1e-6
F32, BF16 = jnp.float32, jnp.bfloat16
NT = (((1,), (1,)), ((), ()))


def _dot(a, b):
    return jnp.dot(a, b, preferred_element_type=F32)


def _gelu_and_grad(u):
    k0, k1 = 0.7978845608028654, 0.044715
    u2 = u * u
    t = jnp.tanh(k0 * (u + k1 * (u2 * u)))
    cdf = 0.5 * (1.0 + t)
    grad = cdf + (0.5 * u) * (1.0 - t * t) * (k0 + (3.0 * k0 * k1) * u2)
    return u * cdf, grad


def _kernel(
    n, side, share, ids_hbm, emb_ref, gain_hbm, w_in_ref, w_out_ref, d_out_hbm,
    out_ref, d_tab, d_w_in_ref, d_w_out_ref,
    ids_ref, gain_ref, d_out_ref, emb, emb_sib, w1, w2, first, ring, x_buf, n_buf, nt_buf, dot_buf, y_buf, dn_buf,
    dw, dw_sib, dw_ring, dx,
    load_sem, emb_sem, w_send, w_recv, w_push, w_got, cast_send, cast_recv, look_send, look_recv,
    dw_push, dw_got, dw_send, dw_recv, dx_send, dx_recv, dx_push, dx_got,
):
    rank = lax.axis_index("tp")
    z, c = rank // 2, rank % 2
    peer = 2 * z + (1 - c)
    far = n // 2
    last = n - 1
    hops = (2 * lax.rem(z + 1, n) + c, 2 * lax.rem(z + n - 1, n) + c)
    half, dim = first.shape[2], first.shape[3]
    v_rows, v_pad = emb_ref.shape[0], emb.shape[0]
    lane = ids_ref.shape[2]
    per_half = half // lane

    def send(src, dst, ssem, rsem, to):
        return pltpu.make_async_remote_copy(
            src_ref=src, dst_ref=dst, send_sem=ssem, recv_sem=rsem,
            device_id={"tp": to}, device_id_type=pl.DeviceIdType.MESH,
        )

    def chip(d, k):
        return lax.rem(z + (2 * d - 1) * k + 2 * n, n)

    loads = [
        pltpu.make_async_copy(src, dst, load_sem.at[i])
        for i, (src, dst) in enumerate(
            [
                (ids_hbm, ids_ref),
                (emb_ref, emb.at[pl.ds(0, v_rows)]),
                (w_in_ref, w1.at[rank]),
                (w_out_ref, w2.at[rank]),
                (d_out_hbm, d_out_ref),
                (gain_hbm, gain_ref),
            ]
        )
    ]
    for load in loads:
        load.start()
    emb[v_rows:] = jnp.zeros((v_pad - v_rows, dim), BF16)
    emb_sib[v_rows:] = jnp.zeros((v_pad - v_rows, dim), BF16)

    group = lax.axis_index("dp")
    gx, gy = group // side, group % side
    quarter = (2 * (gx % 2) + gy % 2) if share > 1 else 0
    square = []
    for e in range(1, share):
        px = gx + (e // 2) * (1 - 2 * (gx % 2))
        py = gy + (e % 2) * (1 - 2 * (gy % 2))
        square.append(px * side + py)

    barrier = pltpu.get_barrier_semaphore()
    for other in (*hops, peer):
        pl.semaphore_signal(barrier, inc=1, device_id={"tp": other}, device_id_type=pl.DeviceIdType.MESH)
    for other in square:
        pl.semaphore_signal(barrier, inc=1, device_id={"dp": other}, device_id_type=pl.DeviceIdType.MESH)
    pl.semaphore_wait(barrier, 2 + share)

    def w_part(w, ref):
        size = ref.shape[0] // share
        return ref.at[pl.ds(pl.multiple_of(quarter * size, size), size)]

    def w_block(w, d, m):
        return (w1, w2)[w].at[2 * chip(d, m) + c]

    def w_copy(d, m, w, own=False):
        dst = w_part(w, w_block(w, d, m))
        src = w_part(w, (w_in_ref, w_out_ref)[w]) if own else dst
        return send(src, dst, w_send.at[d, m, w], w_recv.at[d, m, w], hops[d])

    def w_casts(d, m, w):
        part = w_part(w, w_block(w, d, m))
        return [
            pltpu.make_async_remote_copy(
                src_ref=part, dst_ref=part,
                send_sem=cast_send.at[e, d, 2 * (m - 1) + w], recv_sem=cast_recv.at[e, d, 2 * (m - 1) + w],
                device_id={"dp": other}, device_id_type=pl.DeviceIdType.MESH,
            )
            for e, other in enumerate(square)
        ]

    def w_peer(d, m, w, own=False):
        dst = w_block(w, d, m)
        src = (w_in_ref, w_out_ref)[w] if own else dst
        return send(src, dst, w_push.at[d, m, w], w_got.at[d, m, w], peer)

    blocks = [(d, m, w) for m in range(1, far + 1) for d in range(2) for w in range(2) if m < far or w == d]

    def w_stage(m):
        for d, k, w in blocks:
            if k == m:
                w_copy(d, m - 1, w).wait_recv()
                if m < far - 1 or (m == far - 1 and w == d):
                    w_copy(d, m, w).start()
                for copy in w_casts(d, m, w):
                    copy.start()

    def w_share():
        for d, m, w in blocks:
            for copy in w_casts(d, m, w):
                copy.wait_recv()
            w_peer(d, m, w).start()

    emb_copy = send(emb_ref, emb_sib.at[pl.ds(0, v_rows)], emb_sem.at[0], emb_sem.at[1], peer)
    emb_copy.start()
    for d in range(2):
        for w in range(2):
            w_copy(d, 0, w, True).start()
    for w in range(2):
        w_peer(0, 0, w, True).start()

    lanes = lax.broadcasted_iota(jnp.int32, (2 * half, v_pad), 1)

    def wanted(j, h):
        at = (2 * (2 * j + c) + h) * per_half
        return [jnp.broadcast_to(ids_ref[at + i], (lane, lane)).T for i in range(per_half)]

    def pick(want, base):
        want = jnp.concatenate([want - base] * (v_pad // lane), axis=1)
        return jnp.where(want == lanes, 1.0, 0.0).astype(BF16)

    def look_half(d, p):
        return d + (1 - 2 * d) * (p % 2)

    def look_want(p):
        k = far - (p + 1) // 2
        return jnp.concatenate(
            [t for d in range(2) for t in wanted(chip(1 - d, k), look_half(d, p))], axis=0
        )

    def look_copy(d, p):
        return send(first.at[d, p], ring.at[d, p], look_send.at[d, p], look_recv.at[d, p], hops[d])

    def looked_up(want):
        return _dot(pick(want, rank * v_rows), emb[...]) + _dot(pick(want, peer * v_rows), emb_sib[...])

    loads[0].wait()
    loads[1].wait()
    want = look_want(0)
    x_buf[...] = _dot(pick(want, rank * v_rows), emb[...])
    w_stage(1)
    emb_copy.wait_recv()
    part = x_buf[...] + _dot(pick(want, peer * v_rows), emb_sib[...])
    for d in range(2):
        first[d, 0] = part[d * half : (d + 1) * half].astype(BF16)
        look_copy(d, 0).start()
    for load in loads[2:]:
        load.wait()

    def gather_round(p, carry):
        part = looked_up(look_want(p))
        for d in range(2):
            mine = part[d * half : (d + 1) * half]
            first[d, p] = mine.astype(BF16)

            @pl.when(p >= 2)
            def _():
                look_copy(d, p - 2).wait_recv()
                first[d, p] = (first[d, p].astype(F32) + ring[d, p - 2].astype(F32)).astype(BF16)

            look_copy(d, p).start()

        for at, m in ((1, 2), (3, 3), (5, 4)):

            @pl.when(p == at)
            def _():
                w_stage(m)

        @pl.when(p == last - 1)
        def _():
            w_share()

        return carry

    lax.fori_loop(1, last, gather_round, 0)
    x_buf[...] = looked_up(jnp.concatenate([t for h in range(2) for t in wanted(z, h)], axis=0))
    dot_buf[...] = d_out_ref[...].astype(F32).T.astype(BF16)
    y_buf[...] = jnp.zeros_like(y_buf)
    dn_buf[...] = jnp.zeros_like(dn_buf)
    for p in (last - 2, last - 1):
        for d in range(2):
            look_copy(d, p).wait_recv()

    x = x_buf[...] + jnp.concatenate(
        [ring[h, last - 1].astype(F32) + ring[1 - h, last - 2].astype(F32) for h in range(2)], axis=0
    )
    x_buf[...] = x
    inv_rms = lax.rsqrt(jnp.mean(x * x, axis=-1, keepdims=True) + EPS)
    gain = jnp.concatenate([gain_ref[i : i + 1].astype(F32) for i in range(gain_ref.shape[0])], axis=1)
    normed = (x * inv_rms * gain).astype(BF16)
    n_buf[...] = normed
    nt_buf[...] = normed.astype(F32).T.astype(BF16)

    def dw_peer(d, j):
        return send(dw.at[2 * j + (1 - c), d], dw_sib.at[j, d], dw_push.at[d, j], dw_got.at[d, j], peer)

    def dw_where(d, p):
        return chip(1 - d, far - (p + 1) // 2), look_half(d, p)

    def dw_copy(d, p):
        j, h = dw_where(d, p)
        return send(dw.at[2 * j + c, h], dw_ring.at[d, p], dw_send.at[d, p], dw_recv.at[d, p], hops[d])

    def dw_step(p, fresh=False):
        for d in range(2):
            j, h = dw_where(d, p)
            dw_peer(h, j).wait_recv()
            if fresh:
                dw[2 * j + c, h] = dw[2 * j + c, h] + dw_sib[j, h]
            else:
                dw_copy(d, p - 2).wait_recv()
                dw[2 * j + c, h] = (dw[2 * j + c, h] + dw_sib[j, h]) + dw_ring[d, p - 2]
            dw_copy(d, p).start()

    def tile_chip(i):
        return chip(i % 2, far - (i + 1) // 2)

    for d, m, w in blocks:
        w_peer(d, m, w).wait_recv()
    for w in range(2):
        w_peer(0, 0, w, True).wait_recv()

    def mlp(i, carry):
        j = tile_chip(i)
        w1t = jnp.concatenate([w1[2 * j], w1[2 * j + 1]], axis=1)
        w2t = jnp.concatenate([w2[2 * j], w2[2 * j + 1]], axis=0)
        hid = w1.shape[2]
        u = _dot(n_buf[...], w1t).astype(BF16).astype(F32)
        d_h = lax.dot_general(d_out_ref[...], w2t, NT, preferred_element_type=F32).astype(BF16).astype(F32)
        act, grad = _gelu_and_grad(u)
        h = act.astype(BF16)
        d_u = (d_h * grad).astype(BF16)
        y_buf[...] += _dot(h, w2t)
        dn_buf[...] += lax.dot_general(d_u, w1t, NT, preferred_element_type=F32)
        g1 = _dot(nt_buf[...], d_u)
        g2 = _dot(dot_buf[...], h)
        for q in range(2):
            dw[2 * j + q, 0] = g1[:, q * hid : (q + 1) * hid]
            dw[2 * j + q, 1] = g2[:, q * hid : (q + 1) * hid]

        for d in range(2):
            dw_peer(d, j).start()

        for at, p in ((1, 0), (3, 1)):

            @pl.when(i == at)
            def _():
                dw_step(p, fresh=True)

        return carry

    lax.fori_loop(0, n, mlp, 0)

    x = x_buf[...]
    d_scaled = dn_buf[...] * gain
    inv_rms = lax.rsqrt(jnp.mean(x * x, axis=-1, keepdims=True) + EPS)
    row_proj = jnp.mean(d_scaled * x, axis=-1, keepdims=True)
    dx[rank] = (
        d_out_ref[...].astype(F32) + inv_rms * (d_scaled - x * inv_rms * inv_rms * row_proj)
    ).astype(BF16)

    def dx_where(d, p):
        return chip(d, p // 2), d + (1 - 2 * d) * (p % 2)

    def dx_piece(d, p, core):
        j, h = dx_where(d, p)
        return dx.at[2 * j + core, pl.ds(pl.multiple_of(h * half, half), half)]

    def dx_copy(d, p):
        piece = dx_piece(d, p, c)
        return send(piece, piece, dx_send.at[d, p], dx_recv.at[d, p], hops[d])

    def dx_peer(d, p):
        piece = dx_piece(d, p, c)
        return send(piece, piece, dx_push.at[d, p], dx_got.at[d, p], peer)

    v_tile = v_pad // 4

    def add_rows(pieces, fresh=False):
        def tile(v, carry, size=v_tile):
            at = pl.ds(v * v_tile if isinstance(v, int) else pl.multiple_of(v * v_tile, v_tile), size)
            rows = lax.broadcasted_iota(jnp.int32, (size, half), 0)
            total = None if fresh else d_tab[at]
            for d, p, core in pieces:
                j, h = dx_where(d, p)
                i0 = (2 * (2 * j + core) + h) * per_half
                ids = jnp.concatenate([ids_ref[i0 + i] for i in range(per_half)], axis=1)
                place = jnp.where(rows == ids - (rank * v_rows + v * v_tile), 1.0, 0.0).astype(BF16)
                more = _dot(place, dx[2 * j + core, pl.ds(pl.multiple_of(h * half, half), half)])
                total = more if total is None else total + more
            d_tab[at] = total
            return carry

        lax.fori_loop(0, v_rows // v_tile, tile, 0)
        if v_rows % v_tile:
            tile(v_rows // v_tile, 0, v_rows % v_tile)

    for d in range(2):
        dx_copy(d, 0).start()
    for d in range(2):
        dx_copy(d, 1).start()
    for d in range(2):
        dx_peer(d, 0).start()
    out_ref[...] = (x + y_buf[...]).astype(BF16)
    add_rows([(0, 0, c), (1, 0, c)], fresh=True)

    def scatter_round(p, carry):
        for d in range(2):
            dx_copy(d, p - 2).wait_recv()
            dx_copy(d, p).start()
            dx_peer(d, p).start()

        @pl.when(p == 2)
        def _():
            for d in range(2):
                dx_peer(d, 0).wait_recv()

        @pl.when(p > 2)
        def _():
            for d in range(2):
                dx_peer(d, p - 1).wait_recv()

        was = p - 2 + (p + 1) // 4
        add_rows([(0, p, c), (1, p, c), (0, was, 1 - c), (1, was, 1 - c)])
        dw_step(p)
        return carry

    lax.fori_loop(2, last, scatter_round, 0)
    for p in (last, last + 1):
        for d in range(2):
            dx_copy(d, p - 2).wait_recv()
            dx_peer(d, p).start()
        for d in range(2):
            dx_peer(d, p - 1).wait_recv()
        add_rows([(0, p, c), (1, p, c), (0, p - 1, 1 - c), (1, p - 1, 1 - c)])
    for d in range(2):
        dx_peer(d, last + 1).wait_recv()
    add_rows([(0, last + 1, 1 - c), (1, last + 1, 1 - c)])
    sums = []
    for h in range(2):
        dw_peer(h, z).wait_recv()
        sums.append(dw[rank, h] + dw_sib[z, h])
    for d in range(2):
        dw_copy(d, last - 2).wait_recv()
    for d in range(2):
        dw_copy(d, last - 1).wait_recv()
    d_w_in_ref[...] = (sums[0] + dw_ring[1, last - 2]) + dw_ring[0, last - 1]
    d_w_out_ref[...] = ((sums[1] + dw_ring[0, last - 2]) + dw_ring[1, last - 1]).T

    emb_copy.wait_send()
    for d in range(2):
        for w in range(2):
            w_copy(d, 0, w, True).wait_send()
        dx_peer(d, 0).wait_send()
    for w in range(2):
        w_peer(0, 0, w, True).wait_send()
    for d, m, w in blocks:
        if m < far - 1 or (m == far - 1 and w == d):
            w_copy(d, m, w).wait_send()
        w_peer(d, m, w).wait_send()
        for copy in w_casts(d, m, w):
            copy.wait_send()

    def drain(k, carry):
        for d in range(2):
            dw_peer(d, k).wait_send()

            @pl.when(k < last)
            def _():
                look_copy(d, k).wait_send()
                dx_copy(d, k).wait_send()
                dw_copy(d, k).wait_send()

            @pl.when(k > 0)
            def _():
                dx_peer(d, k + 1).wait_send()

        return carry

    lax.fori_loop(0, n, drain, 0)


STORE_IN = pl.BlockSpec(memory_space=pl.ANY)


def _store(*refs):
    copies = [pltpu.make_async_copy(refs[i], refs[4 + i], refs[8].at[i]) for i in range(4)]
    for copy in copies:
        copy.start()
    for copy in copies:
        copy.wait()


def solution(mesh):
    tp = mesh.shape["tp"]
    n = tp // 2
    dp = mesh.shape["dp"]
    side = math.isqrt(dp)
    share = 4 if side * side == dp and side % 2 == 0 else 1

    def shard_step(token_ids, emb_table, norm_gain, w_in, w_out, d_out):
        v_rows, dim = emb_table.shape
        hid = w_out.shape[0]
        rows = d_out.shape[0]
        half = rows // 2
        lane = min(128, half)
        v_pad = -(-v_rows // 512) * 512
        vmem = pl.BlockSpec(memory_space=pltpu.VMEM)
        hbm = pl.BlockSpec(memory_space=pl.ANY)
        dma = pltpu.SemaphoreType.DMA
        results = pl.pallas_call(
            functools.partial(_kernel, n, side, share),
            out_shape=(
                pltpu.VMEM((rows, dim), BF16),
                pltpu.VMEM((v_rows, dim), F32),
                pltpu.VMEM((dim, hid), F32),
                pltpu.VMEM((hid, dim), F32),
            ),
            in_specs=[hbm] * 6,
            out_specs=(vmem,) * 4,
            scratch_shapes=[
                pltpu.VMEM((token_ids.shape[0] // lane, 1, lane), jnp.int32),
                pltpu.VMEM((dim // 128, 128), BF16),
                pltpu.VMEM((rows, dim), BF16),
                pltpu.VMEM((v_pad, dim), BF16),
                pltpu.VMEM((v_pad, dim), BF16),
                pltpu.VMEM((tp, dim, hid), BF16),
                pltpu.VMEM((tp, hid, dim), BF16),
                pltpu.VMEM((2, n - 1, half, dim), BF16),
                pltpu.VMEM((2, n - 1, half, dim), BF16),
                pltpu.VMEM((rows, dim), F32),
                pltpu.VMEM((rows, dim), BF16),
                pltpu.VMEM((dim, rows), BF16),
                pltpu.VMEM((dim, rows), BF16),
                pltpu.VMEM((rows, dim), F32),
                pltpu.VMEM((rows, dim), F32),
                pltpu.VMEM((tp, 2, dim, hid), F32),
                pltpu.VMEM((n, 2, dim, hid), F32),
                pltpu.VMEM((2, n - 1, dim, hid), F32),
                pltpu.VMEM((tp, rows, dim), BF16),
                dma((6,)),
                dma((2,)),
                dma((2, n // 2, 2)), dma((2, n // 2, 2)), dma((2, n // 2 + 1, 2)), dma((2, n // 2 + 1, 2)),
                dma((max(share - 1, 1), 2, n)), dma((max(share - 1, 1), 2, n)),
                dma((2, n - 1)), dma((2, n - 1)),
                dma((2, n)), dma((2, n)), dma((2, n - 1)), dma((2, n - 1)),
                dma((2, n - 1)), dma((2, n - 1)), dma((2, n + 1)), dma((2, n + 1)),
            ],
            compiler_params=pltpu.CompilerParams(
                collective_id=0, has_side_effects=True, vmem_limit_bytes=57 * 1024 * 1024
            ),
            name="block_step",
        )(token_ids.reshape(-1, 1, lane), emb_table, norm_gain.reshape(-1, 128), w_in, w_out, d_out)
        return pl.pallas_call(
            _store,
            out_shape=tuple(jax.ShapeDtypeStruct(r.shape, r.dtype) for r in results),
            in_specs=[STORE_IN] * 4,
            out_specs=(hbm,) * 4,
            scratch_shapes=[dma((4,))],
            compiler_params=pltpu.CompilerParams(vmem_limit_bytes=1024 * 1024),
            name="store",
        )(*results)

    return jax.shard_map(
        shard_step,
        mesh=mesh,
        in_specs=(P("dp"), P("tp", None), P(None), P(None, "tp"), P("tp", None), P(("dp", "tp"), None)),
        out_specs=(P(("dp", "tp"), None), P(("dp", "tp"), None), P("dp", "tp"), P(("dp", "tp"), None)),
        check_vma=False,
    )
```

time: 557 us -> 149 us (0.27)
  waiting for transfers between devices: 388 us -> 0 us
  Pallas kernels: 0 us -> 148 us
  other arithmetic: 69.8 us -> 0 us
  matrix products: 48 us -> 0 us
  local copies, waits for them, and re-layouts: 35.6 us -> 0 us
  between operations: 14.2 us -> 0.8 us
    reduce_scatter x3 -> x0, waiting for transfers between devices: 250 us -> none  [the longest x1 96.7 us: shard_step(): mlp_out = lax.psum_scatter(mlp_part, 'tp', scatter_dimension=0, tiled=True)]
    pallas_call x0 -> x2, Pallas kernels: none -> 148 us  [the longest x1 146 us: shard_step(): pl.pallas_call(functools.partial(_kernel, n, side, share), out_shape=(plt...]
    all_gather x3 -> x0, waiting for transfers between devices: 137 us -> none  [the longest x1 53.9 us: shard_step(): normed = lax.all_gather(normed_local, 'tp', axis=0, tiled=True)]
    scatter-add x1 -> x0, other arithmetic: 52.3 us -> none  [shard_step(): jax.ops.segment_sum(d_emb_full.astype(jnp.float32), target_rows, num_segm...]
    dot_general x6 -> x0, matrix products: 48 us -> none  [the longest x1 10.3 us: shard_step(): mlp_part = jnp.dot(hidden, w_out, preferred_element_type=jnp.float32)]
    gather x1 -> x0, local copies, waits for them, and re-layouts: 33.7 us -> none  [shard_step(): table_rows = jnp.take(emb_table, jnp.where(is_owned, local_ids, 0), axis=0)]
    select_n x2 -> x0, other arithmetic: 8.95 us -> none  [the longest x1 8.17 us: shard_step(): jnp.where(is_owned[:, None], table_rows, jnp.zeros((), table_rows.dtype))]
  transfers between devices with their start and end apart: 6 -> 0, of which waited for: 6 -> 0; matrix products, arithmetic and copies ran while one was open for 6% -> 0% of each run, Pallas kernels for 0% -> 0%
where the time goes in v2:
time: 149 us
  Pallas kernels  148 us (99%)
    pallas_call x1, Pallas kernels, shard_step(): pl.pallas_call(functools.partial(_kernel, n, side, share), out_shape=(plt...  146 us

profile of v2, /device:TPU:21, one launch (start us, length us, event | category | flops | bytes accessed | tf_op | source)
XLA Modules:
  0.0 148.8 jit_solution(6195847754624747551)
XLA Ops:
  0.6 145.7 %block_step.1 = (bf16[512,512]{1,0:T(8,128)(2,1)S(1)}, f32[2008,512]{1,0:T(8,128)S(1)}, f32[512,128]{1,0:T(8,128)S(1)}, f32[128,512]{1,0:T(8,128)S(1)}) custom-call(s32[64,1,128]{2,1,0:T(1,128)} %bitcast.2, bf16[2008,512]{1,0:T(8,128)(2,1)} %emb_ref.1, bf16[4,128]{1,0:T(4,128)(2,1)} %bitcast.3, bf16[512,128]{1,0:T(8,128)(2,1)} %w_in_ref.1, ...), custom_call_target="tpu_custom_call" | custom-call | tf_op jit(solution)/shard_map/block_step/pallas_call | solution.py:443
  146.3 2.3 %store.1 = (bf16[512,512]{1,0:T(8,128)(2,1)}, f32[2008,512]{1,0:T(8,128)}, f32[512,128]{1,0:T(8,128)}, f32[128,512]{1,0:T(8,128)}) custom-call(bf16[512,512]{1,0:T(8,128)(2,1)S(1)} %get-tuple-element.8.refs_0_, f32[2008,512]{1,0:T(8,128)S(1)} %get-tuple-element.9.refs_1_, f32[512,128]{1,0:T(8,128)S(1)} %get-tuple-element.10.refs_2_, ...), custom_call_target="tpu_custom_call" | custom-call | tf_op jit(solution)/shard_map/store/pallas_call | solution.py:486

commit v3 on v2

--- a/solution.py
+++ b/solution.py
@@ -29,9 +29,9 @@
 def _kernel(
     n, side, share, ids_hbm, emb_ref, gain_hbm, w_in_ref, w_out_ref, d_out_hbm,
     out_ref, d_tab, d_w_in_ref, d_w_out_ref,
-    ids_ref, gain_ref, d_out_ref, emb, emb_sib, w1, w2, first, ring, x_buf, n_buf, nt_buf, dot_buf, y_buf, dn_buf,
+    ids_ref, gain_ref, d_out_ref, emb, look_out, look_in, w1, w2, first, ring, x_buf, n_buf, nt_buf, dot_buf, y_buf, dn_buf,
     dw, dw_sib, dw_ring, dx,
-    load_sem, emb_sem, w_send, w_recv, w_push, w_got, cast_send, cast_recv, look_send, look_recv,
+    load_sem, w_send, w_recv, w_push, w_got, cast_send, cast_recv, look_send, look_recv, look_push, look_got,
     dw_push, dw_got, dw_send, dw_recv, dx_send, dx_recv, dx_push, dx_got,
 ):
     rank = lax.axis_index("tp")
@@ -70,7 +70,6 @@
     for load in loads:
         load.start()
     emb[v_rows:] = jnp.zeros((v_pad - v_rows, dim), BF16)
-    emb_sib[v_rows:] = jnp.zeros((v_pad - v_rows, dim), BF16)
 
     group = lax.axis_index("dp")
     gx, gy = group // side, group % side
@@ -86,8 +85,6 @@
         pl.semaphore_signal(barrier, inc=1, device_id={"tp": other}, device_id_type=pl.DeviceIdType.MESH)
     for other in square:
         pl.semaphore_signal(barrier, inc=1, device_id={"dp": other}, device_id_type=pl.DeviceIdType.MESH)
-    pl.semaphore_wait(barrier, 2 + share)
-
     def w_part(w, ref):
         size = ref.shape[0] // share
         return ref.at[pl.ds(pl.multiple_of(quarter * size, size), size)]
@@ -133,57 +130,65 @@
                 copy.wait_recv()
             w_peer(d, m, w).start()
 
-    emb_copy = send(emb_ref, emb_sib.at[pl.ds(0, v_rows)], emb_sem.at[0], emb_sem.at[1], peer)
-    emb_copy.start()
+    lanes = lax.broadcasted_iota(jnp.int32, (2 * half, v_pad), 1)
+
+    def wanted(j, h, core):
+        at = (2 * (2 * j + core) + h) * per_half
+        return [jnp.broadcast_to(ids_ref[at + i], (lane, lane)).T for i in range(per_half)]
+
+    def look_half(d, p):
+        return d + (1 - 2 * d) * (p % 2)
+
+    def looked_up(p, core):
+        k = far - (p + 1) // 2
+        want = jnp.concatenate(
+            [t for d in range(2) for t in wanted(chip(1 - d, k), look_half(d, p), core)], axis=0
+        )
+        want = jnp.concatenate([want - rank * v_rows] * (v_pad // lane), axis=1)
+        return _dot(jnp.where(want == lanes, 1.0, 0.0).astype(BF16), emb[...])
+
+    def look_peer(slot):
+        return send(look_out.at[slot], look_in.at[slot], look_push.at[slot], look_got.at[slot], peer)
+
+    def for_peer(slot):
+        part = looked_up(slot + slot // last, 1 - c).astype(BF16)
+        for d in range(2):
+            look_out[slot, d] = part[d * half : (d + 1) * half]
+
+    def look_copy(d, p):
+        return send(first.at[d, p], ring.at[d, p], look_send.at[d, p], look_recv.at[d, p], hops[d])
+
+    loads[0].wait()
+    loads[1].wait()
+    for_peer(0)
+    pl.semaphore_wait(barrier, 2 + share)
+    look_peer(0).start()
     for d in range(2):
         for w in range(2):
             w_copy(d, 0, w, True).start()
     for w in range(2):
         w_peer(0, 0, w, True).start()
-
-    lanes = lax.broadcasted_iota(jnp.int32, (2 * half, v_pad), 1)
-
-    def wanted(j, h):
-        at = (2 * (2 * j + c) + h) * per_half
-        return [jnp.broadcast_to(ids_ref[at + i], (lane, lane)).T for i in range(per_half)]
-
-    def pick(want, base):
-        want = jnp.concatenate([want - base] * (v_pad // lane), axis=1)
-        return jnp.where(want == lanes, 1.0, 0.0).astype(BF16)
-
-    def look_half(d, p):
-        return d + (1 - 2 * d) * (p % 2)
-
-    def look_want(p):
-        k = far - (p + 1) // 2
-        return jnp.concatenate(
-            [t for d in range(2) for t in wanted(chip(1 - d, k), look_half(d, p))], axis=0
-        )
-
-    def look_copy(d, p):
-        return send(first.at[d, p], ring.at[d, p], look_send.at[d, p], look_recv.at[d, p], hops[d])
-
-    def looked_up(want):
-        return _dot(pick(want, rank * v_rows), emb[...]) + _dot(pick(want, peer * v_rows), emb_sib[...])
-
-    loads[0].wait()
-    loads[1].wait()
-    want = look_want(0)
-    x_buf[...] = _dot(pick(want, rank * v_rows), emb[...])
-    w_stage(1)
-    emb_copy.wait_recv()
-    part = x_buf[...] + _dot(pick(want, peer * v_rows), emb_sib[...])
-    for d in range(2):
-        first[d, 0] = part[d * half : (d + 1) * half].astype(BF16)
+    x_buf[...] = looked_up(0, c)
+    look_peer(0).wait_recv()
+    for d in range(2):
+        first[d, 0] = (x_buf[pl.ds(d * half, half)] + look_in[0, d].astype(F32)).astype(BF16)
         look_copy(d, 0).start()
+    for_peer(1)
+    look_peer(1).start()
     for load in loads[2:]:
         load.wait()
 
     def gather_round(p, carry):
-        part = looked_up(look_want(p))
-        for d in range(2):
-            mine = part[d * half : (d + 1) * half]
-            first[d, p] = mine.astype(BF16)
+        x_buf[...] = looked_up(p, c)
+        for m in range(1, far + 1):
+
+            @pl.when(p == m)
+            def _():
+                w_stage(m)
+
+        look_peer(p).wait_recv()
+        for d in range(2):
+            first[d, p] = (x_buf[pl.ds(d * half, half)] + look_in[p, d].astype(F32)).astype(BF16)
 
             @pl.when(p >= 2)
             def _():
@@ -192,20 +197,18 @@
 
             look_copy(d, p).start()
 
-        for at, m in ((1, 2), (3, 3), (5, 4)):
-
-            @pl.when(p == at)
-            def _():
-                w_stage(m)
-
-        @pl.when(p == last - 1)
+        @pl.when(p == far + 1)
         def _():
             w_share()
 
+        for_peer(p + 1)
+        look_peer(p + 1).start()
         return carry
 
     lax.fori_loop(1, last, gather_round, 0)
-    x_buf[...] = looked_up(jnp.concatenate([t for h in range(2) for t in wanted(z, h)], axis=0))
+    x_buf[...] = looked_up(n, c)
+    look_peer(last).wait_recv()
+    x_buf[...] = x_buf[...] + jnp.concatenate([look_in[last, h] for h in range(2)], axis=0).astype(F32)
     dot_buf[...] = d_out_ref[...].astype(F32).T.astype(BF16)
     y_buf[...] = jnp.zeros_like(y_buf)
     dn_buf[...] = jnp.zeros_like(dn_buf)
@@ -358,28 +361,16 @@
         return carry
 
     lax.fori_loop(2, last, scatter_round, 0)
-    for p in (last, last + 1):
+    def finish(p):
         for d in range(2):
             dx_copy(d, p - 2).wait_recv()
             dx_peer(d, p).start()
         for d in range(2):
             dx_peer(d, p - 1).wait_recv()
         add_rows([(0, p, c), (1, p, c), (0, p - 1, 1 - c), (1, p - 1, 1 - c)])
-    for d in range(2):
-        dx_peer(d, last + 1).wait_recv()
-    add_rows([(0, last + 1, 1 - c), (1, last + 1, 1 - c)])
-    sums = []
-    for h in range(2):
-        dw_peer(h, z).wait_recv()
-        sums.append(dw[rank, h] + dw_sib[z, h])
-    for d in range(2):
-        dw_copy(d, last - 2).wait_recv()
-    for d in range(2):
-        dw_copy(d, last - 1).wait_recv()
-    d_w_in_ref[...] = (sums[0] + dw_ring[1, last - 2]) + dw_ring[0, last - 1]
-    d_w_out_ref[...] = ((sums[1] + dw_ring[0, last - 2]) + dw_ring[1, last - 1]).T
-
-    emb_copy.wait_send()
+
+    finish(last)
+
     for d in range(2):
         for w in range(2):
             w_copy(d, 0, w, True).wait_send()
@@ -394,22 +385,44 @@
             copy.wait_send()
 
     def drain(k, carry):
+        look_peer(k).wait_send()
         for d in range(2):
             dw_peer(d, k).wait_send()
 
             @pl.when(k < last)
             def _():
                 look_copy(d, k).wait_send()
+
+            @pl.when(k < last - 2)
+            def _():
                 dx_copy(d, k).wait_send()
                 dw_copy(d, k).wait_send()
-
-            @pl.when(k > 0)
-            def _():
-                dx_peer(d, k + 1).wait_send()
+                dx_peer(d, k + 2).wait_send()
 
         return carry
 
     lax.fori_loop(0, n, drain, 0)
+
+    finish(last + 1)
+    for d in range(2):
+        dx_peer(d, last + 1).wait_recv()
+    add_rows([(0, last + 1, 1 - c), (1, last + 1, 1 - c)])
+    sums = []
+    for h in range(2):
+        dw_peer(h, z).wait_recv()
+        sums.append(dw[rank, h] + dw_sib[z, h])
+    for d in range(2):
+        dw_copy(d, last - 2).wait_recv()
+    for d in range(2):
+        dw_copy(d, last - 1).wait_recv()
+    d_w_in_ref[...] = (sums[0] + dw_ring[1, last - 2]) + dw_ring[0, last - 1]
+    d_w_out_ref[...] = ((sums[1] + dw_ring[0, last - 2]) + dw_ring[1, last - 1]).T
+
+    for d in range(2):
+        for p in (last - 2, last - 1):
+            dx_copy(d, p).wait_send()
+            dw_copy(d, p).wait_send()
+            dx_peer(d, p + 2).wait_send()
 
 
 STORE_IN = pl.BlockSpec(memory_space=pl.ANY)
@@ -455,7 +468,8 @@
                 pltpu.VMEM((dim // 128, 128), BF16),
                 pltpu.VMEM((rows, dim), BF16),
                 pltpu.VMEM((v_pad, dim), BF16),
-                pltpu.VMEM((v_pad, dim), BF16),
+                pltpu.VMEM((n, 2, half, dim), BF16),
+                pltpu.VMEM((n, 2, half, dim), BF16),
                 pltpu.VMEM((tp, dim, hid), BF16),
                 pltpu.VMEM((tp, hid, dim), BF16),
                 pltpu.VMEM((2, n - 1, half, dim), BF16),
@@ -471,10 +485,9 @@
                 pltpu.VMEM((2, n - 1, dim, hid), F32),
                 pltpu.VMEM((tp, rows, dim), BF16),
                 dma((6,)),
-                dma((2,)),
                 dma((2, n // 2, 2)), dma((2, n // 2, 2)), dma((2, n // 2 + 1, 2)), dma((2, n // 2 + 1, 2)),
                 dma((max(share - 1, 1), 2, n)), dma((max(share - 1, 1), 2, n)),
-                dma((2, n - 1)), dma((2, n - 1)),
+                dma((2, n - 1)), dma((2, n - 1)), dma((n,)), dma((n,)),
                 dma((2, n)), dma((2, n)), dma((2, n - 1)), dma((2, n - 1)),
                 dma((2, n - 1)), dma((2, n - 1)), dma((2, n + 1)), dma((2, n + 1)),
             ],

time: 149 us -> 147 us (0.987)
  Pallas kernels: 148 us -> 146 us
    pallas_call x1, Pallas kernels: 146 us -> 143 us  [shard_step(): pl.pallas_call(functools.partial(_kernel, n, side, share), out_shape=(plt...]
where the time goes in v3:
time: 147 us
  Pallas kernels  146 us (99%)
    pallas_call x1, Pallas kernels, shard_step(): pl.pallas_call(functools.partial(_kernel, n, side, share), out_shape=(plt...  143 us

profile of v3, /device:TPU:21, one launch (start us, length us, event | category | flops | bytes accessed | tf_op | source)
XLA Modules:
  0.0 146.5 jit_solution(6634260862548891192)
XLA Ops:
  0.6 143.4 %block_step.1 = (bf16[512,512]{1,0:T(8,128)(2,1)S(1)}, f32[2008,512]{1,0:T(8,128)S(1)}, f32[512,128]{1,0:T(8,128)S(1)}, f32[128,512]{1,0:T(8,128)S(1)}) custom-call(s32[64,1,128]{2,1,0:T(1,128)} %bitcast.2, bf16[2008,512]{1,0:T(8,128)(2,1)} %emb_ref.1, bf16[4,128]{1,0:T(4,128)(2,1)} %bitcast.3, bf16[512,128]{1,0:T(8,128)(2,1)} %w_in_ref.1, ...), custom_call_target="tpu_custom_call" | custom-call | tf_op jit(solution)/shard_map/block_step/pallas_call | solution.py:456
  144.0 2.3 %store.1 = (bf16[512,512]{1,0:T(8,128)(2,1)}, f32[2008,512]{1,0:T(8,128)}, f32[512,128]{1,0:T(8,128)}, f32[128,512]{1,0:T(8,128)}) custom-call(bf16[512,512]{1,0:T(8,128)(2,1)S(1)} %get-tuple-element.8.refs_0_, f32[2008,512]{1,0:T(8,128)S(1)} %get-tuple-element.9.refs_1_, f32[512,128]{1,0:T(8,128)S(1)} %get-tuple-element.10.refs_2_, ...), custom_call_target="tpu_custom_call" | custom-call | tf_op jit(solution)/shard_map/store/pallas_call | solution.py:499

commit v4 on v3

--- a/solution.py
+++ b/solution.py
@@ -95,14 +95,14 @@
     def w_copy(d, m, w, own=False):
         dst = w_part(w, w_block(w, d, m))
         src = w_part(w, (w_in_ref, w_out_ref)[w]) if own else dst
-        return send(src, dst, w_send.at[d, m, w], w_recv.at[d, m, w], hops[d])
+        return send(src, dst, w_send.at[0], w_recv.at[d, m], hops[d])
 
     def w_casts(d, m, w):
         part = w_part(w, w_block(w, d, m))
         return [
             pltpu.make_async_remote_copy(
                 src_ref=part, dst_ref=part,
-                send_sem=cast_send.at[e, d, 2 * (m - 1) + w], recv_sem=cast_recv.at[e, d, 2 * (m - 1) + w],
+                send_sem=cast_send.at[e], recv_sem=cast_recv.at[e],
                 device_id={"dp": other}, device_id_type=pl.DeviceIdType.MESH,
             )
             for e, other in enumerate(square)
@@ -111,23 +111,29 @@
     def w_peer(d, m, w, own=False):
         dst = w_block(w, d, m)
         src = (w_in_ref, w_out_ref)[w] if own else dst
-        return send(src, dst, w_push.at[d, m, w], w_got.at[d, m, w], peer)
+        return send(src, dst, w_push.at[0], w_got.at[0], peer)
 
     blocks = [(d, m, w) for m in range(1, far + 1) for d in range(2) for w in range(2) if m < far or w == d]
 
+    def bulk(parts):
+        rows = parts * w2.shape[1] // share
+        return dx.at[0, pl.ds(0, rows)] if rows <= dx.shape[1] else w2.at[pl.ds(0, parts)]
+
     def w_stage(m):
+        for d in range(2):
+            came = bulk(2 if m < far else 1)
+            send(came, came, w_send.at[0], w_recv.at[d, m - 1], hops[d]).wait_recv()
         for d, k, w in blocks:
             if k == m:
-                w_copy(d, m - 1, w).wait_recv()
                 if m < far - 1 or (m == far - 1 and w == d):
                     w_copy(d, m, w).start()
                 for copy in w_casts(d, m, w):
                     copy.start()
 
     def w_share():
+        for e in range(share - 1):
+            send(bulk(2 * last), bulk(2 * last), cast_send.at[e], cast_recv.at[e], peer).wait_recv()
         for d, m, w in blocks:
-            for copy in w_casts(d, m, w):
-                copy.wait_recv()
             w_peer(d, m, w).start()
 
     lanes = lax.broadcasted_iota(jnp.int32, (2 * half, v_pad), 1)
@@ -137,7 +143,9 @@
         return [jnp.broadcast_to(ids_ref[at + i], (lane, lane)).T for i in range(per_half)]
 
     def look_half(d, p):
-        return d + (1 - 2 * d) * (p % 2)
+        if isinstance(p, int) and p == 0:
+            return 1 - d
+        return (p + 1) % 2 + d * (p // last)
 
     def looked_up(p, core):
         k = far - (p + 1) // 2
@@ -148,15 +156,15 @@
         return _dot(jnp.where(want == lanes, 1.0, 0.0).astype(BF16), emb[...])
 
     def look_peer(slot):
-        return send(look_out.at[slot], look_in.at[slot], look_push.at[slot], look_got.at[slot], peer)
+        return send(look_out.at[slot], look_in.at[slot], look_push.at[0], look_got.at[slot], peer)
 
     def for_peer(slot):
-        part = looked_up(slot + slot // last, 1 - c).astype(BF16)
+        part = looked_up(slot, 1 - c).astype(BF16)
         for d in range(2):
             look_out[slot, d] = part[d * half : (d + 1) * half]
 
     def look_copy(d, p):
-        return send(first.at[d, p], ring.at[d, p], look_send.at[d, p], look_recv.at[d, p], hops[d])
+        return send(first.at[d, p], ring.at[d, p], look_send.at[0], look_recv.at[d, p], hops[d])
 
     loads[0].wait()
     loads[1].wait()
@@ -190,11 +198,18 @@
         for d in range(2):
             first[d, p] = (x_buf[pl.ds(d * half, half)] + look_in[p, d].astype(F32)).astype(BF16)
 
-            @pl.when(p >= 2)
+            @pl.when(p > 2 if d else p >= 2)
             def _():
                 look_copy(d, p - 2).wait_recv()
                 first[d, p] = (first[d, p].astype(F32) + ring[d, p - 2].astype(F32)).astype(BF16)
 
+            if d:
+
+                @pl.when(p == 1)
+                def _():
+                    look_copy(d, 0).wait_recv()
+                    first[d, p] = (first[d, p].astype(F32) + ring[d, 0].astype(F32)).astype(BF16)
+
             look_copy(d, p).start()
 
         @pl.when(p == far + 1)
@@ -206,38 +221,38 @@
         return carry
 
     lax.fori_loop(1, last, gather_round, 0)
-    x_buf[...] = looked_up(n, c)
+    x_buf[...] = looked_up(last, c)
     look_peer(last).wait_recv()
     x_buf[...] = x_buf[...] + jnp.concatenate([look_in[last, h] for h in range(2)], axis=0).astype(F32)
-    dot_buf[...] = d_out_ref[...].astype(F32).T.astype(BF16)
+    for h in range(2):
+        dot_buf[h] = d_out_ref[pl.ds(h * half, half)].astype(F32).T.astype(BF16)
     y_buf[...] = jnp.zeros_like(y_buf)
     dn_buf[...] = jnp.zeros_like(dn_buf)
-    for p in (last - 2, last - 1):
+    gain = jnp.concatenate([gain_ref[i : i + 1].astype(F32) for i in range(gain_ref.shape[0])], axis=1)
+
+    def norm(h):
+        p = last - 2 + h
+        at = pl.ds(h * half, half)
         for d in range(2):
             look_copy(d, p).wait_recv()
-
-    x = x_buf[...] + jnp.concatenate(
-        [ring[h, last - 1].astype(F32) + ring[1 - h, last - 2].astype(F32) for h in range(2)], axis=0
-    )
-    x_buf[...] = x
-    inv_rms = lax.rsqrt(jnp.mean(x * x, axis=-1, keepdims=True) + EPS)
-    gain = jnp.concatenate([gain_ref[i : i + 1].astype(F32) for i in range(gain_ref.shape[0])], axis=1)
-    normed = (x * inv_rms * gain).astype(BF16)
-    n_buf[...] = normed
-    nt_buf[...] = normed.astype(F32).T.astype(BF16)
+        x = x_buf[at] + (ring[0, p].astype(F32) + ring[1, p].astype(F32))
+        x_buf[at] = x
+        normed = (x * lax.rsqrt(jnp.mean(x * x, axis=-1, keepdims=True) + EPS) * gain).astype(BF16)
+        n_buf[at] = normed
+        nt_buf[h] = normed.astype(F32).T.astype(BF16)
 
     def dw_peer(d, j):
-        return send(dw.at[2 * j + (1 - c), d], dw_sib.at[j, d], dw_push.at[d, j], dw_got.at[d, j], peer)
+        return send(dw.at[2 * j + (1 - c), d], dw_sib.at[j, d], dw_push.at[0], dw_got.at[d, j], peer)
 
     def dw_where(d, p):
-        return chip(1 - d, far - (p + 1) // 2), look_half(d, p)
+        return chip(1 - d, far - (p + 1) // 2), d + (1 - 2 * d) * (p % 2)
 
     def dw_copy(d, p):
         j, h = dw_where(d, p)
-        return send(dw.at[2 * j + c, h], dw_ring.at[d, p], dw_send.at[d, p], dw_recv.at[d, p], hops[d])
-
-    def dw_step(p, fresh=False):
-        for d in range(2):
+        return send(dw.at[2 * j + c, h], dw_ring.at[d, p], dw_send.at[0], dw_recv.at[d, p], hops[d])
+
+    def dw_step(p, fresh=False, ways=(0, 1)):
+        for d in ways:
             j, h = dw_where(d, p)
             dw_peer(h, j).wait_recv()
             if fresh:
@@ -250,31 +265,34 @@
     def tile_chip(i):
         return chip(i % 2, far - (i + 1) // 2)
 
-    for d, m, w in blocks:
-        w_peer(d, m, w).wait_recv()
-    for w in range(2):
-        w_peer(0, 0, w, True).wait_recv()
-
-    def mlp(i, carry):
+    send(w1, w1, w_push.at[0], w_got.at[0], peer).wait_recv()
+
+    def mlp(i, h):
+        at = pl.ds(h * half, half)
         j = tile_chip(i)
         w1t = jnp.concatenate([w1[2 * j], w1[2 * j + 1]], axis=1)
         w2t = jnp.concatenate([w2[2 * j], w2[2 * j + 1]], axis=0)
         hid = w1.shape[2]
-        u = _dot(n_buf[...], w1t).astype(BF16).astype(F32)
-        d_h = lax.dot_general(d_out_ref[...], w2t, NT, preferred_element_type=F32).astype(BF16).astype(F32)
+        u = _dot(n_buf[at], w1t).astype(BF16).astype(F32)
+        d_h = lax.dot_general(d_out_ref[at], w2t, NT, preferred_element_type=F32).astype(BF16).astype(F32)
         act, grad = _gelu_and_grad(u)
-        h = act.astype(BF16)
+        hidden = act.astype(BF16)
         d_u = (d_h * grad).astype(BF16)
-        y_buf[...] += _dot(h, w2t)
-        dn_buf[...] += lax.dot_general(d_u, w1t, NT, preferred_element_type=F32)
-        g1 = _dot(nt_buf[...], d_u)
-        g2 = _dot(dot_buf[...], h)
-        for q in range(2):
-            dw[2 * j + q, 0] = g1[:, q * hid : (q + 1) * hid]
-            dw[2 * j + q, 1] = g2[:, q * hid : (q + 1) * hid]
-
-        for d in range(2):
-            dw_peer(d, j).start()
+        y_buf[at] += _dot(hidden, w2t)
+        dn_buf[at] += lax.dot_general(d_u, w1t, NT, preferred_element_type=F32)
+        for which, g in ((0, _dot(nt_buf[h], d_u)), (1, _dot(dot_buf[h], hidden))):
+            for q in range(2):
+                piece = g[:, q * hid : (q + 1) * hid]
+                dw[2 * j + q, which] = piece if h == 0 else dw[2 * j + q, which] + piece
+
+    def first_half(i, carry):
+        mlp(i, 0)
+        return carry
+
+    def second_half(i, carry):
+        mlp(i, 1)
+        for d in range(2):
+            dw_peer(d, tile_chip(i)).start()
 
         for at, p in ((1, 0), (3, 1)):
 
@@ -284,30 +302,34 @@
 
         return carry
 
-    lax.fori_loop(0, n, mlp, 0)
-
-    x = x_buf[...]
-    d_scaled = dn_buf[...] * gain
-    inv_rms = lax.rsqrt(jnp.mean(x * x, axis=-1, keepdims=True) + EPS)
-    row_proj = jnp.mean(d_scaled * x, axis=-1, keepdims=True)
-    dx[rank] = (
-        d_out_ref[...].astype(F32) + inv_rms * (d_scaled - x * inv_rms * inv_rms * row_proj)
-    ).astype(BF16)
+    def leave(h):
+        at = pl.ds(h * half, half)
+        x = x_buf[at]
+        d_scaled = dn_buf[at] * gain
+        inv_rms = lax.rsqrt(jnp.mean(x * x, axis=-1, keepdims=True) + EPS)
+        row_proj = jnp.mean(d_scaled * x, axis=-1, keepdims=True)
+        dx[rank, at] = (
+            d_out_ref[at].astype(F32) + inv_rms * (d_scaled - x * inv_rms * inv_rms * row_proj)
+        ).astype(BF16)
+        for d in range(2):
+            dx_copy(d, h).start()
+        dx_peer(h, h).start()
+        out_ref[at] = (x + y_buf[at]).astype(BF16)
 
     def dx_where(d, p):
-        return chip(d, p // 2), d + (1 - 2 * d) * (p % 2)
+        return chip(d, p // 2), p % 2 + d * (p // n)
 
     def dx_piece(d, p, core):
         j, h = dx_where(d, p)
         return dx.at[2 * j + core, pl.ds(pl.multiple_of(h * half, half), half)]
 
     def dx_copy(d, p):
-        piece = dx_piece(d, p, c)
-        return send(piece, piece, dx_send.at[d, p], dx_recv.at[d, p], hops[d])
+        piece = dx_piece(d, p + d * (p // (last - 1)), c)
+        return send(piece, piece, dx_send.at[0], dx_recv.at[d, p], hops[d])
 
     def dx_peer(d, p):
         piece = dx_piece(d, p, c)
-        return send(piece, piece, dx_push.at[d, p], dx_got.at[d, p], peer)
+        return send(piece, piece, dx_push.at[0], dx_got.at[d, p], peer)
 
     v_tile = v_pad // 4
 
@@ -330,14 +352,14 @@
         if v_rows % v_tile:
             tile(v_rows // v_tile, 0, v_rows % v_tile)
 
-    for d in range(2):
-        dx_copy(d, 0).start()
-    for d in range(2):
-        dx_copy(d, 1).start()
-    for d in range(2):
-        dx_peer(d, 0).start()
-    out_ref[...] = (x + y_buf[...]).astype(BF16)
-    add_rows([(0, 0, c), (1, 0, c)], fresh=True)
+    norm(0)
+    lax.fori_loop(0, n, first_half, 0)
+    leave(0)
+    norm(1)
+    lax.fori_loop(0, n, second_half, 0)
+    leave(1)
+    dw_step(2)
+    add_rows([(0, 0, c), (0, 1, c)], fresh=True)
 
     def scatter_round(p, carry):
         for d in range(2):
@@ -348,62 +370,38 @@
         @pl.when(p == 2)
         def _():
             for d in range(2):
-                dx_peer(d, 0).wait_recv()
+                dx_peer(d, d).wait_recv()
 
         @pl.when(p > 2)
         def _():
             for d in range(2):
                 dx_peer(d, p - 1).wait_recv()
 
-        was = p - 2 + (p + 1) // 4
-        add_rows([(0, p, c), (1, p, c), (0, was, 1 - c), (1, was, 1 - c)])
-        dw_step(p)
+        add_rows([(0, p, c), (1, p, c), (0, (p - 1) * ((p + 1) // 4), 1 - c), (1, p - 1, 1 - c)])
+
+        @pl.when(p > 2)
+        def _():
+            dw_step(p)
+
         return carry
 
-    lax.fori_loop(2, last, scatter_round, 0)
-    def finish(p):
+    lax.fori_loop(2, last - 1, scatter_round, 0)
+
+    def finish(p, ways):
         for d in range(2):
             dx_copy(d, p - 2).wait_recv()
+            if d in ways:
+                dx_copy(d, last - 1).start()
             dx_peer(d, p).start()
         for d in range(2):
             dx_peer(d, p - 1).wait_recv()
         add_rows([(0, p, c), (1, p, c), (0, p - 1, 1 - c), (1, p - 1, 1 - c)])
-
-    finish(last)
-
-    for d in range(2):
-        for w in range(2):
-            w_copy(d, 0, w, True).wait_send()
-        dx_peer(d, 0).wait_send()
-    for w in range(2):
-        w_peer(0, 0, w, True).wait_send()
-    for d, m, w in blocks:
-        if m < far - 1 or (m == far - 1 and w == d):
-            w_copy(d, m, w).wait_send()
-        w_peer(d, m, w).wait_send()
-        for copy in w_casts(d, m, w):
-            copy.wait_send()
-
-    def drain(k, carry):
-        look_peer(k).wait_send()
-        for d in range(2):
-            dw_peer(d, k).wait_send()
-
-            @pl.when(k < last)
-            def _():
-                look_copy(d, k).wait_send()
-
-            @pl.when(k < last - 2)
-            def _():
-                dx_copy(d, k).wait_send()
-                dw_copy(d, k).wait_send()
-                dx_peer(d, k + 2).wait_send()
-
-        return carry
-
-    lax.fori_loop(0, n, drain, 0)
-
-    finish(last + 1)
+        if ways:
+            dw_step(last - 1, ways=ways)
+
+    finish(last - 1, (0,))
+    finish(last, (1,))
+    finish(last + 1, ())
     for d in range(2):
         dx_peer(d, last + 1).wait_recv()
     add_rows([(0, last + 1, 1 - c), (1, last + 1, 1 - c)])
@@ -418,11 +416,18 @@
     d_w_in_ref[...] = (sums[0] + dw_ring[1, last - 2]) + dw_ring[0, last - 1]
     d_w_out_ref[...] = ((sums[1] + dw_ring[0, last - 2]) + dw_ring[1, last - 1]).T
 
-    for d in range(2):
-        for p in (last - 2, last - 1):
-            dx_copy(d, p).wait_send()
-            dw_copy(d, p).wait_send()
-            dx_peer(d, p + 2).wait_send()
+    for copy in (
+        send(first, ring, look_send.at[0], look_recv.at[0, 0], peer),
+        send(look_out, look_in, look_push.at[0], look_got.at[0], peer),
+        send(w1, w1, w_push.at[0], w_got.at[0], peer),
+        send(dw_sib, dw_sib, dw_push.at[0], dw_got.at[0, 0], peer),
+        send(dw_ring, dw_ring, dw_send.at[0], dw_recv.at[0, 0], peer),
+        send(ring, ring, dx_send.at[0], dx_recv.at[0, 0], peer),
+        send(look_in, look_in, dx_push.at[0], dx_got.at[0, 0], peer),
+        send(bulk(2 * last), bulk(2 * last), w_send.at[0], w_recv.at[0, 0], peer),
+        *[send(bulk(2 * last), bulk(2 * last), cast_send.at[e], cast_recv.at[e], peer) for e in range(share - 1)],
+    ):
+        copy.wait_send()
 
 
 STORE_IN = pl.BlockSpec(memory_space=pl.ANY)
@@ -476,8 +481,8 @@
                 pltpu.VMEM((2, n - 1, half, dim), BF16),
                 pltpu.VMEM((rows, dim), F32),
                 pltpu.VMEM((rows, dim), BF16),
-                pltpu.VMEM((dim, rows), BF16),
-                pltpu.VMEM((dim, rows), BF16),
+                pltpu.VMEM((2, dim, half), BF16),
+                pltpu.VMEM((2, dim, half), BF16),
                 pltpu.VMEM((rows, dim), F32),
                 pltpu.VMEM((rows, dim), F32),
                 pltpu.VMEM((tp, 2, dim, hid), F32),
@@ -485,11 +490,11 @@
                 pltpu.VMEM((2, n - 1, dim, hid), F32),
                 pltpu.VMEM((tp, rows, dim), BF16),
                 dma((6,)),
-                dma((2, n // 2, 2)), dma((2, n // 2, 2)), dma((2, n // 2 + 1, 2)), dma((2, n // 2 + 1, 2)),
-                dma((max(share - 1, 1), 2, n)), dma((max(share - 1, 1), 2, n)),
-                dma((2, n - 1)), dma((2, n - 1)), dma((n,)), dma((n,)),
-                dma((2, n)), dma((2, n)), dma((2, n - 1)), dma((2, n - 1)),
-                dma((2, n - 1)), dma((2, n - 1)), dma((2, n + 1)), dma((2, n + 1)),
+                dma((1,)), dma((2, n // 2)), dma((1,)), dma((1,)),
+                dma((max(share - 1, 1),)), dma((max(share - 1, 1),)),
+                dma((1,)), dma((2, n - 1)), dma((1,)), dma((n,)),
+                dma((1,)), dma((2, n)), dma((1,)), dma((2, n - 1)),
+                dma((1,)), dma((2, n - 1)), dma((1,)), dma((2, n + 1)),
             ],
             compiler_params=pltpu.CompilerParams(
                 collective_id=0, has_side_effects=True, vmem_limit_bytes=57 * 1024 * 1024

time: 147 us -> 142 us (0.966)
  Pallas kernels: 146 us -> 141 us
    pallas_call x1, Pallas kernels: 143 us -> 139 us  [shard_step(): pl.pallas_call(functools.partial(_kernel, n, side, share), out_shape=(plt...]
where the time goes in v4:
time: 142 us
  Pallas kernels  141 us (99%)
    pallas_call x1, Pallas kernels, shard_step(): pl.pallas_call(functools.partial(_kernel, n, side, share), out_shape=(plt...  139 us

profile of v4, /device:TPU:21, one launch (start us, length us, event | category | flops | bytes accessed | tf_op | source)
XLA Modules:
  0.0 141.8 jit_solution(9888861312629187593)
XLA Ops:
  0.6 138.6 %block_step.1 = (bf16[512,512]{1,0:T(8,128)(2,1)S(1)}, f32[2008,512]{1,0:T(8,128)S(1)}, f32[512,128]{1,0:T(8,128)S(1)}, f32[128,512]{1,0:T(8,128)S(1)}) custom-call(s32[64,1,128]{2,1,0:T(1,128)} %bitcast.2, bf16[2008,512]{1,0:T(8,128)(2,1)} %emb_ref.1, bf16[4,128]{1,0:T(4,128)(2,1)} %bitcast.3, bf16[512,128]{1,0:T(8,128)(2,1)} %w_in_ref.1, ...), custom_call_target="tpu_custom_call" | custom-call | tf_op jit(solution)/shard_map/block_step/pallas_call | solution.py:461
  139.3 2.3 %store.1 = (bf16[512,512]{1,0:T(8,128)(2,1)}, f32[2008,512]{1,0:T(8,128)}, f32[512,128]{1,0:T(8,128)}, f32[128,512]{1,0:T(8,128)}) custom-call(bf16[512,512]{1,0:T(8,128)(2,1)S(1)} %get-tuple-element.8.refs_0_, f32[2008,512]{1,0:T(8,128)S(1)} %get-tuple-element.9.refs_1_, f32[512,128]{1,0:T(8,128)S(1)} %get-tuple-element.10.refs_2_, ...), custom_call_target="tpu_custom_call" | custom-call | tf_op jit(solution)/shard_map/store/pallas_call | solution.py:504

commit v5 on v4

--- a/solution.py
+++ b/solution.py
@@ -29,7 +29,7 @@
 def _kernel(
     n, side, share, ids_hbm, emb_ref, gain_hbm, w_in_ref, w_out_ref, d_out_hbm,
     out_ref, d_tab, d_w_in_ref, d_w_out_ref,
-    ids_ref, gain_ref, d_out_ref, emb, look_out, look_in, w1, w2, first, ring, x_buf, n_buf, nt_buf, dot_buf, y_buf, dn_buf,
+    ids_ref, gain_ref, d_out_ref, emb, look_out, look_in, w1, w2, first, ring, x_buf, n_buf, nt_buf, dot_buf, dh_buf, h_buf, du_buf, y_buf, dn_buf,
     dw, dw_sib, dw_ring, dx,
     load_sem, w_send, w_recv, w_push, w_got, cast_send, cast_recv, look_send, look_recv, look_push, look_got,
     dw_push, dw_got, dw_send, dw_recv, dx_send, dx_recv, dx_push, dx_got,
@@ -171,18 +171,18 @@
     for_peer(0)
     pl.semaphore_wait(barrier, 2 + share)
     look_peer(0).start()
-    for d in range(2):
-        for w in range(2):
-            w_copy(d, 0, w, True).start()
-    for w in range(2):
-        w_peer(0, 0, w, True).start()
     x_buf[...] = looked_up(0, c)
     look_peer(0).wait_recv()
     for d in range(2):
         first[d, 0] = (x_buf[pl.ds(d * half, half)] + look_in[0, d].astype(F32)).astype(BF16)
         look_copy(d, 0).start()
+    for d in range(2):
+        for w in range(2):
+            w_copy(d, 0, w, True).start()
     for_peer(1)
     look_peer(1).start()
+    for w in range(2):
+        w_peer(0, 0, w, True).start()
     for load in loads[2:]:
         load.wait()
 
@@ -190,7 +190,7 @@
         x_buf[...] = looked_up(p, c)
         for m in range(1, far + 1):
 
-            @pl.when(p == m)
+            @pl.when(p == m + 1)
             def _():
                 w_stage(m)
 
@@ -212,7 +212,7 @@
 
             look_copy(d, p).start()
 
-        @pl.when(p == far + 1)
+        @pl.when(p == last - 1)
         def _():
             w_share()
 
@@ -224,8 +224,7 @@
     x_buf[...] = looked_up(last, c)
     look_peer(last).wait_recv()
     x_buf[...] = x_buf[...] + jnp.concatenate([look_in[last, h] for h in range(2)], axis=0).astype(F32)
-    for h in range(2):
-        dot_buf[h] = d_out_ref[pl.ds(h * half, half)].astype(F32).T.astype(BF16)
+    dot_buf[...] = d_out_ref[...].astype(F32).T.astype(BF16)
     y_buf[...] = jnp.zeros_like(y_buf)
     dn_buf[...] = jnp.zeros_like(dn_buf)
     gain = jnp.concatenate([gain_ref[i : i + 1].astype(F32) for i in range(gain_ref.shape[0])], axis=1)
@@ -239,7 +238,7 @@
         x_buf[at] = x
         normed = (x * lax.rsqrt(jnp.mean(x * x, axis=-1, keepdims=True) + EPS) * gain).astype(BF16)
         n_buf[at] = normed
-        nt_buf[h] = normed.astype(F32).T.astype(BF16)
+        nt_buf[:, pl.ds(h * half, half)] = normed.astype(F32).T.astype(BF16)
 
     def dw_peer(d, j):
         return send(dw.at[2 * j + (1 - c), d], dw_sib.at[j, d], dw_push.at[0], dw_got.at[d, j], peer)
@@ -267,32 +266,45 @@
 
     send(w1, w1, w_push.at[0], w_got.at[0], peer).wait_recv()
 
-    def mlp(i, h):
-        at = pl.ds(h * half, half)
+    def weights(i):
         j = tile_chip(i)
         w1t = jnp.concatenate([w1[2 * j], w1[2 * j + 1]], axis=1)
         w2t = jnp.concatenate([w2[2 * j], w2[2 * j + 1]], axis=0)
+        return j, w1t, w2t
+
+    def hidden_grad(i, h):
+        out_grad = d_out_ref[pl.ds(h * half, half)]
+        return lax.dot_general(out_grad, weights(i)[2], NT, preferred_element_type=F32).astype(BF16)
+
+    def early(i, carry):
+        dh_buf[i] = hidden_grad(i, 0)
+        return carry
+
+    def inner(i, h, d_h):
+        at = pl.ds(h * half, half)
+        w1t = weights(i)[1]
+        act, grad = _gelu_and_grad(_dot(n_buf[at], w1t).astype(BF16).astype(F32))
+        hidden = act.astype(BF16)
+        d_u = (d_h.astype(F32) * grad).astype(BF16)
+        dn_buf[at] += lax.dot_general(d_u, w1t, NT, preferred_element_type=F32)
+        return hidden, d_u
+
+    def first_half(i, carry):
+        h_buf[i], du_buf[i] = inner(i, 0, dh_buf[i])
+        return carry
+
+    def second_half(i, carry):
+        j, _, w2t = weights(i)
         hid = w1.shape[2]
-        u = _dot(n_buf[at], w1t).astype(BF16).astype(F32)
-        d_h = lax.dot_general(d_out_ref[at], w2t, NT, preferred_element_type=F32).astype(BF16).astype(F32)
-        act, grad = _gelu_and_grad(u)
-        hidden = act.astype(BF16)
-        d_u = (d_h * grad).astype(BF16)
-        y_buf[at] += _dot(hidden, w2t)
-        dn_buf[at] += lax.dot_general(d_u, w1t, NT, preferred_element_type=F32)
-        for which, g in ((0, _dot(nt_buf[h], d_u)), (1, _dot(dot_buf[h], hidden))):
+        hidden, d_u = inner(i, 1, hidden_grad(i, 1))
+        hidden = jnp.concatenate([h_buf[i], hidden], axis=0)
+        d_u = jnp.concatenate([du_buf[i], d_u], axis=0)
+        for which, g in ((0, _dot(nt_buf[...], d_u)), (1, _dot(dot_buf[...], hidden))):
             for q in range(2):
-                piece = g[:, q * hid : (q + 1) * hid]
-                dw[2 * j + q, which] = piece if h == 0 else dw[2 * j + q, which] + piece
-
-    def first_half(i, carry):
-        mlp(i, 0)
-        return carry
-
-    def second_half(i, carry):
-        mlp(i, 1)
-        for d in range(2):
-            dw_peer(d, tile_chip(i)).start()
+                dw[2 * j + q, which] = g[:, q * hid : (q + 1) * hid]
+        for d in range(2):
+            dw_peer(d, j).start()
+        y_buf[...] += _dot(hidden, w2t)
 
         for at, p in ((1, 0), (3, 1)):
 
@@ -314,7 +326,6 @@
         for d in range(2):
             dx_copy(d, h).start()
         dx_peer(h, h).start()
-        out_ref[at] = (x + y_buf[at]).astype(BF16)
 
     def dx_where(d, p):
         return chip(d, p // 2), p % 2 + d * (p // n)
@@ -352,12 +363,14 @@
         if v_rows % v_tile:
             tile(v_rows // v_tile, 0, v_rows % v_tile)
 
+    lax.fori_loop(0, n, early, 0)
     norm(0)
     lax.fori_loop(0, n, first_half, 0)
     leave(0)
     norm(1)
     lax.fori_loop(0, n, second_half, 0)
     leave(1)
+    out_ref[...] = (x_buf[...] + y_buf[...]).astype(BF16)
     dw_step(2)
     add_rows([(0, 0, c), (0, 1, c)], fresh=True)
 
@@ -389,13 +402,14 @@
 
     def finish(p, ways):
         for d in range(2):
+            dx_peer(d, p - 1).wait_recv()
+        add_rows([(0, p - 1, 1 - c), (1, p - 1, 1 - c)])
+        for d in range(2):
             dx_copy(d, p - 2).wait_recv()
             if d in ways:
                 dx_copy(d, last - 1).start()
             dx_peer(d, p).start()
-        for d in range(2):
-            dx_peer(d, p - 1).wait_recv()
-        add_rows([(0, p, c), (1, p, c), (0, p - 1, 1 - c), (1, p - 1, 1 - c)])
+        add_rows([(0, p, c), (1, p, c)])
         if ways:
             dw_step(last - 1, ways=ways)
 
@@ -481,8 +495,11 @@
                 pltpu.VMEM((2, n - 1, half, dim), BF16),
                 pltpu.VMEM((rows, dim), F32),
                 pltpu.VMEM((rows, dim), BF16),
-                pltpu.VMEM((2, dim, half), BF16),
-                pltpu.VMEM((2, dim, half), BF16),
+                pltpu.VMEM((dim, rows), BF16),
+                pltpu.VMEM((dim, rows), BF16),
+                pltpu.VMEM((n, half, 2 * hid), BF16),
+                pltpu.VMEM((n, half, 2 * hid), BF16),
+                pltpu.VMEM((n, half, 2 * hid), BF16),
                 pltpu.VMEM((rows, dim), F32),
                 pltpu.VMEM((rows, dim), F32),
                 pltpu.VMEM((tp, 2, dim, hid), F32),

time: 142 us -> 145 us (1.021)
  Pallas kernels: 141 us -> 144 us
    pallas_call x1, Pallas kernels: 139 us -> 141 us  [shard_step(): pl.pallas_call(functools.partial(_kernel, n, side, share), out_shape=(plt...]
where the time goes in v5:
time: 145 us; the launch traced here: 144 us
  Pallas kernels  144 us (99%)
    pallas_call x1, Pallas kernels, shard_step(): pl.pallas_call(functools.partial(_kernel, n, side, share), out_shape=(plt...  141 us

profile of v5, /device:TPU:21, one launch (start us, length us, event | category | flops | bytes accessed | tf_op | source)
XLA Modules:
  0.0 144.4 jit_solution(4649245095783841506)
XLA Ops:
  0.6 141.3 %block_step.1 = (bf16[512,512]{1,0:T(8,128)(2,1)S(1)}, f32[2008,512]{1,0:T(8,128)S(1)}, f32[512,128]{1,0:T(8,128)S(1)}, f32[128,512]{1,0:T(8,128)S(1)}) custom-call(s32[64,1,128]{2,1,0:T(1,128)} %bitcast.2, bf16[2008,512]{1,0:T(8,128)(2,1)} %emb_ref.1, bf16[4,128]{1,0:T(4,128)(2,1)} %bitcast.3, bf16[512,128]{1,0:T(8,128)(2,1)} %w_in_ref.1, ...), custom_call_target="tpu_custom_call" | custom-call | tf_op jit(solution)/shard_map/block_step/pallas_call | solution.py:475
  141.9 2.3 %store.1 = (bf16[512,512]{1,0:T(8,128)(2,1)}, f32[2008,512]{1,0:T(8,128)}, f32[512,128]{1,0:T(8,128)}, f32[128,512]{1,0:T(8,128)}) custom-call(bf16[512,512]{1,0:T(8,128)(2,1)S(1)} %get-tuple-element.8.refs_0_, f32[2008,512]{1,0:T(8,128)S(1)} %get-tuple-element.9.refs_1_, f32[512,128]{1,0:T(8,128)S(1)} %get-tuple-element.10.refs_2_, ...), custom_call_target="tpu_custom_call" | custom-call | tf_op jit(solution)/shard_map/store/pallas_call | solution.py:521

commit v6 on v5

--- a/solution.py
+++ b/solution.py
@@ -171,18 +171,18 @@
     for_peer(0)
     pl.semaphore_wait(barrier, 2 + share)
     look_peer(0).start()
+    for d in range(2):
+        for w in range(2):
+            w_copy(d, 0, w, True).start()
+    for w in range(2):
+        w_peer(0, 0, w, True).start()
     x_buf[...] = looked_up(0, c)
     look_peer(0).wait_recv()
     for d in range(2):
         first[d, 0] = (x_buf[pl.ds(d * half, half)] + look_in[0, d].astype(F32)).astype(BF16)
         look_copy(d, 0).start()
-    for d in range(2):
-        for w in range(2):
-            w_copy(d, 0, w, True).start()
     for_peer(1)
     look_peer(1).start()
-    for w in range(2):
-        w_peer(0, 0, w, True).start()
     for load in loads[2:]:
         load.wait()
 
@@ -190,7 +190,7 @@
         x_buf[...] = looked_up(p, c)
         for m in range(1, far + 1):
 
-            @pl.when(p == m + 1)
+            @pl.when(p == m)
             def _():
                 w_stage(m)
 
@@ -212,7 +212,7 @@
 
             look_copy(d, p).start()
 
-        @pl.when(p == last - 1)
+        @pl.when(p == far + 1)
         def _():
             w_share()
 
@@ -277,7 +277,8 @@
         return lax.dot_general(out_grad, weights(i)[2], NT, preferred_element_type=F32).astype(BF16)
 
     def early(i, carry):
-        dh_buf[i] = hidden_grad(i, 0)
+        for t in (2 * i, 2 * i + 1):
+            dh_buf[t] = hidden_grad(t, 0)
         return carry
 
     def inner(i, h, d_h):
@@ -286,17 +287,21 @@
         act, grad = _gelu_and_grad(_dot(n_buf[at], w1t).astype(BF16).astype(F32))
         hidden = act.astype(BF16)
         d_u = (d_h.astype(F32) * grad).astype(BF16)
-        dn_buf[at] += lax.dot_general(d_u, w1t, NT, preferred_element_type=F32)
-        return hidden, d_u
+        return hidden, d_u, lax.dot_general(d_u, w1t, NT, preferred_element_type=F32)
 
     def first_half(i, carry):
-        h_buf[i], du_buf[i] = inner(i, 0, dh_buf[i])
+        total = dn_buf[:half]
+        for t in (2 * i, 2 * i + 1):
+            h_buf[t], du_buf[t], more = inner(t, 0, dh_buf[t])
+            total = total + more
+        dn_buf[:half] = total
         return carry
 
     def second_half(i, carry):
         j, _, w2t = weights(i)
         hid = w1.shape[2]
-        hidden, d_u = inner(i, 1, hidden_grad(i, 1))
+        hidden, d_u, more = inner(i, 1, hidden_grad(i, 1))
+        dn_buf[half:] += more
         hidden = jnp.concatenate([h_buf[i], hidden], axis=0)
         d_u = jnp.concatenate([du_buf[i], d_u], axis=0)
         for which, g in ((0, _dot(nt_buf[...], d_u)), (1, _dot(dot_buf[...], hidden))):
@@ -363,9 +368,9 @@
         if v_rows % v_tile:
             tile(v_rows // v_tile, 0, v_rows % v_tile)
 
-    lax.fori_loop(0, n, early, 0)
+    lax.fori_loop(0, n // 2, early, 0)
     norm(0)
-    lax.fori_loop(0, n, first_half, 0)
+    lax.fori_loop(0, n // 2, first_half, 0)
     leave(0)
     norm(1)
     lax.fori_loop(0, n, second_half, 0)

time: 145 us -> 140 us (0.966)
  Pallas kernels: 144 us -> 139 us
    pallas_call x1, Pallas kernels: 141 us -> 136 us  [shard_step(): pl.pallas_call(functools.partial(_kernel, n, side, share), out_shape=(plt...]
where the time goes in v6:
time: 140 us
  Pallas kernels  139 us (99%)
    pallas_call x1, Pallas kernels, shard_step(): pl.pallas_call(functools.partial(_kernel, n, side, share), out_shape=(plt...  136 us

profile of v6, /device:TPU:21, one launch (start us, length us, event | category | flops | bytes accessed | tf_op | source)
XLA Modules:
  0.0 139.6 jit_solution(12722667820868391736)
XLA Ops:
  0.6 136.4 %block_step.1 = (bf16[512,512]{1,0:T(8,128)(2,1)S(1)}, f32[2008,512]{1,0:T(8,128)S(1)}, f32[512,128]{1,0:T(8,128)S(1)}, f32[128,512]{1,0:T(8,128)S(1)}) custom-call(s32[64,1,128]{2,1,0:T(1,128)} %bitcast.2, bf16[2008,512]{1,0:T(8,128)(2,1)} %emb_ref.1, bf16[4,128]{1,0:T(4,128)(2,1)} %bitcast.3, bf16[512,128]{1,0:T(8,128)(2,1)} %w_in_ref.1, ...), custom_call_target="tpu_custom_call" | custom-call | tf_op jit(solution)/shard_map/block_step/pallas_call | solution.py:480
  137.1 2.3 %store.1 = (bf16[512,512]{1,0:T(8,128)(2,1)}, f32[2008,512]{1,0:T(8,128)}, f32[512,128]{1,0:T(8,128)}, f32[128,512]{1,0:T(8,128)}) custom-call(bf16[512,512]{1,0:T(8,128)(2,1)S(1)} %get-tuple-element.8.refs_0_, f32[2008,512]{1,0:T(8,128)S(1)} %get-tuple-element.9.refs_1_, f32[512,128]{1,0:T(8,128)S(1)} %get-tuple-element.10.refs_2_, ...), custom_call_target="tpu_custom_call" | custom-call | tf_op jit(solution)/shard_map/store/pallas_call | solution.py:526

commit v7 on v6

--- a/solution.py
+++ b/solution.py
@@ -291,7 +291,7 @@
 
     def first_half(i, carry):
         total = dn_buf[:half]
-        for t in (2 * i, 2 * i + 1):
+        for t in (4 * i, 4 * i + 1, 4 * i + 2, 4 * i + 3):
             h_buf[t], du_buf[t], more = inner(t, 0, dh_buf[t])
             total = total + more
         dn_buf[:half] = total
@@ -370,7 +370,7 @@
 
     lax.fori_loop(0, n // 2, early, 0)
     norm(0)
-    lax.fori_loop(0, n // 2, first_half, 0)
+    lax.fori_loop(0, n // 4, first_half, 0)
     leave(0)
     norm(1)
     lax.fori_loop(0, n, second_half, 0)

time: 140 us -> 140 us (level)
  no operation moved by 1% of the time
where the time goes in v7:
time: 140 us
  Pallas kernels  139 us (99%)
    pallas_call x1, Pallas kernels, shard_step(): pl.pallas_call(functools.partial(_kernel, n, side, share), out_shape=(plt...  137 us

profile of v7, /device:TPU:21, one launch (start us, length us, event | category | flops | bytes accessed | tf_op | source)
XLA Modules:
  0.0 139.9 jit_solution(10132438565574454760)
XLA Ops:
  0.6 136.8 %block_step.1 = (bf16[512,512]{1,0:T(8,128)(2,1)S(1)}, f32[2008,512]{1,0:T(8,128)S(1)}, f32[512,128]{1,0:T(8,128)S(1)}, f32[128,512]{1,0:T(8,128)S(1)}) custom-call(s32[64,1,128]{2,1,0:T(1,128)} %bitcast.2, bf16[2008,512]{1,0:T(8,128)(2,1)} %emb_ref.1, bf16[4,128]{1,0:T(4,128)(2,1)} %bitcast.3, bf16[512,128]{1,0:T(8,128)(2,1)} %w_in_ref.1, ...), custom_call_target="tpu_custom_call" | custom-call | tf_op jit(solution)/shard_map/block_step/pallas_call | solution.py:480
  137.4 2.3 %store.1 = (bf16[512,512]{1,0:T(8,128)(2,1)}, f32[2008,512]{1,0:T(8,128)}, f32[512,128]{1,0:T(8,128)}, f32[128,512]{1,0:T(8,128)}) custom-call(bf16[512,512]{1,0:T(8,128)(2,1)S(1)} %get-tuple-element.8.refs_0_, f32[2008,512]{1,0:T(8,128)S(1)} %get-tuple-element.9.refs_1_, f32[512,128]{1,0:T(8,128)S(1)} %get-tuple-element.10.refs_2_, ...), custom_call_target="tpu_custom_call" | custom-call | tf_op jit(solution)/shard_map/store/pallas_call | solution.py:526
